TPU v7x, 8 devices: a whole 2x2x1 slice. The times are simulated.
8 devices in a mesh: pod: 1 (over z), data: 2 (over y), tensor: 4 (over x, core).
Axes of the slice: x: 2, y: 2, z: 1, core: 2. Of those that a mesh axis runs over, the one named last changes fastest.
Arguments:
- token_ids: int32 [8192], P(('pod', 'data'))
- embed_table: bfloat16 [151936, 896], P('tensor')
- norm_gain: bfloat16 [896], replicated
- w_in: bfloat16 [896, 4864], P(None, 'tensor')
- w_out: bfloat16 [4864, 896], P('tensor')
- d_out: bfloat16 [8192, 896], P(('pod', 'data', 'tensor'))
Outputs:
- output 1: bfloat16 [8192, 896], P(('pod', 'data', 'tensor'))
- output 2: float32 [151936, 896], P(('pod', 'tensor'))
- output 3: float32 [896, 4864], P('pod', 'tensor')
- output 4: float32 [4864, 896], P(('pod', 'tensor'))
All inputs are finite; a program needn't handle non-finite values.
Results may differ from a plain program's by a relative error of at most 0.00578052.
Values are sent between devices in bfloat16 or wider.
A program may use at most 1 GiB of HBM per device.

v0:
```python
import jax
import jax.numpy as jnp
from jax import lax
from jax.sharding import PartitionSpec as P

NORM_EPS = 1e-6


def gelu_tanh(value):
    return jax.nn.gelu(value, approximate=True)


def solution(mesh):
    tok_spec = P(("pod", "data", "tensor"), None)

    def per_device(token_ids, embed_table, norm_gain, w_in, w_out, d_out):
        shard_rows = embed_table.shape[0]
        tp_rank = lax.axis_index("tensor")
        local_ids = token_ids - tp_rank * shard_rows
        is_owned = (local_ids >= 0) & (local_ids < shard_rows)
        picked = jnp.take(embed_table, jnp.where(is_owned, local_ids, 0), axis=0)
        partial_rows = jnp.where(is_owned[:, None], picked, jnp.zeros_like(picked))
        embedded = lax.psum_scatter(partial_rows, "tensor", scatter_dimension=0, tiled=True)
        gain_f32 = norm_gain.astype(jnp.float32)
        x_f32 = embedded.astype(jnp.float32)
        inv_rms = lax.rsqrt(jnp.mean(x_f32 * x_f32, axis=-1, keepdims=True) + NORM_EPS)
        x_hat = x_f32 * inv_rms
        normed = (x_hat * gain_f32).astype(jnp.bfloat16)
        normed_all = lax.all_gather(normed, "tensor", axis=0, tiled=True)
        pre_gelu = jnp.dot(normed_all, w_in, preferred_element_type=jnp.float32).astype(jnp.bfloat16)
        hidden_f32, gelu_pull = jax.vjp(gelu_tanh, pre_gelu.astype(jnp.float32))
        hidden = hidden_f32.astype(jnp.bfloat16)
        mlp_part = jnp.dot(hidden, w_out, preferred_element_type=jnp.float32)
        mlp_out = lax.psum_scatter(mlp_part, "tensor", scatter_dimension=0, tiled=True)
        block_out = (x_f32 + mlp_out).astype(jnp.bfloat16)

        grad_all = lax.all_gather(d_out, "tensor", axis=0, tiled=True)
        grad_hidden = lax.dot_general(grad_all, w_out, (((1,), (1,)), ((), ())), preferred_element_type=jnp.float32)
        grad_pre = gelu_pull(grad_hidden)[0].astype(jnp.bfloat16)
        grad_w_out = lax.dot_general(hidden, grad_all, (((0,), (0,)), ((), ())), preferred_element_type=jnp.float32)
        grad_w_in = lax.dot_general(normed_all, grad_pre, (((0,), (0,)), ((), ())), preferred_element_type=jnp.float32)
        norm_part = lax.dot_general(grad_pre, w_in, (((1,), (1,)), ((), ())), preferred_element_type=jnp.float32)
        d_normed = lax.psum_scatter(norm_part, "tensor", scatter_dimension=0, tiled=True)
        d_hat = d_normed * gain_f32
        d_norm_in = inv_rms * (d_hat - x_hat * jnp.mean(d_hat * x_hat, axis=-1, keepdims=True))
        d_embed = (d_out.astype(jnp.float32) + d_norm_in).astype(jnp.bfloat16)
        d_embed_all = lax.all_gather(d_embed, "tensor", axis=0, tiled=True)
        grad_table = jax.ops.segment_sum(d_embed_all.astype(jnp.float32), jnp.where(is_owned, local_ids, shard_rows), num_segments=shard_rows)
        grad_table = lax.psum(grad_table, "data")
        grad_w_in = lax.psum(grad_w_in, "data")
        grad_w_out = lax.psum(grad_w_out, "data")
        return block_out, grad_table, grad_w_in, grad_w_out

    return jax.shard_map(
        per_device,
        mesh=mesh,
        in_specs=(P(("pod", "data")), P("tensor", None), P(None), P(None, "tensor"), P("tensor", None), tok_spec),
        out_specs=(tok_spec, P(("pod", "tensor"), None), P("pod", "tensor"), P(("pod", "tensor"), None)),
        check_vma=False,
    )
```

profile of v0, /device:TPU:0, one launch (start us, length us, event | category | flops | bytes accessed | tf_op | source)
XLA Modules:
  0.0 4487.3 jit_solution(17631465582843956422)
XLA Ops:
  7.2 0.9 compare_and_fusion.1
  8.1 1.3 subtract_select_fusion
  9.4 126.7 %gather_fusion = bf16[4096,896]{1,0:T(8,128)(2,1)} fusion(bf16[37984,896]{1,0:T(8,128)(2,1)} %param.7, s32[4096]{0:T(1024)S(1)} %get-tuple-element.9), kind=kCustom, calls=%fused_computation | custom fusion | bytes 14696448 | tf_op jit(solution)/shard_map/jit(_take)/gather | solution.py:21
  136.1 7.1 select_select_fusion
  143.3 126.7 %reduce-scatter.4.cloned.1.call-done = bf16[1024,896]{1,0:T(8,128)(2,1)} async-done(((bf16[4096,896]{1,0:T(8,128)(2,1)}), bf16[1024,896]{1,0:T(8,128)(2,1)}) %reduce-scatter.4.cloned.1.call-update) | async-done | bytes 1835024 | tf_op jit(solution)/shard_map/reduce_scatter | solution.py:23
  270.0 1.9 fusion.19
  271.9 3.2 fusion.13
  275.2 0.7 all-gather.6.cloned.1.call-update
  275.9 0.2 reduce-scatter.8.cloned.1.call-start
  276.1 48.7 %all-gather.4.cloned.1.call-done = bf16[4096,896]{1,0:T(8,128)(2,1)} async-done(((bf16[1024,896]{1,0:T(8,128)(2,1)}), bf16[4096,896]{1,0:T(8,128)(2,1)}) %all-gather.4.cloned.1.call-update) | async-done | bytes 7340048 | tf_op jit(solution)/shard_map/all_gather | solution.py:29
  324.9 15.8 convolution_convert_fusion
  340.6 35.3 all-gather.6.cloned.1.call-done
  376.0 25.6 fusion.3
  401.6 3.7 copy-done.7
  405.3 14.4 fusion.26
  419.7 1.5 copy-done.6
  421.3 21.8 fusion.24
  443.1 0.3 all-gather.8.cloned.1.call-start
  443.4 84.8 %reduce-scatter.8.cloned.1.call-done = f32[1024,896]{1,0:T(8,128)} async-done(((f32[4096,896]{1,0:T(8,128)}), f32[1024,896]{1,0:T(8,128)}) %reduce-scatter.8.cloned.1.call-update) | async-done | bytes 3670032 | tf_op jit(solution)/shard_map/reduce_scatter | solution.py:43
  528.3 2.8 fusion.14
  531.1 108.0 %reduce-scatter.6.cloned.1.call-done = f32[1024,896]{1,0:T(8,128)} async-done(((f32[4096,896]{1,0:T(8,128)}), f32[1024,896]{1,0:T(8,128)}) %reduce-scatter.6.cloned.1.call-update) | async-done | bytes 3670032 | tf_op jit(solution)/shard_map/reduce_scatter | solution.py:34
  639.1 5.6 fusion.18
  644.8 16.5 fusion.27
  661.4 18.1 fusion.22
  679.5 15.0 all-gather.8.cloned.1.call-done
  694.5 9.8 convert_element_type.43
  704.3 43.4 broadcast_in_dim.42
  747.7 611.0 %scatter_fusion = f32[37984,896]{1,0:T(8,128)} fusion(f32[37984,896]{1,0:T(8,128)} %broadcast_in_dim.42, s32[4096]{0:T(1024)S(1)} %copy-done.4, f32[4096,896]{1,0:T(8,128)} %convert_element_type.43), kind=kCustom, calls=%fused_computation.1 | custom fusion | flops 3670016 | bytes 44056576 | tf_op jit(solution)/shard_map/scatter-add | solution.py:48
  1358.8 3024.9 %all-reduce.4.cloned.1.call-done = f32[37984,896]{1,0:T(8,128)} async-done(((f32[37984,896]{1,0:T(8,128)}), f32[37984,896]{1,0:T(8,128)}) %all-reduce.4.cloned.1.call-update) | async-done | bytes 136134672 | tf_op jit(solution)/shard_map/psum | solution.py:49
  4383.6 90.1 %copy.14 = f32[37984,896]{1,0:T(8,128)} copy(f32[37984,896]{1,0:T(8,128)} %all-reduce.4.cloned.1.call-done) | data formatting | bytes 272269312
  4473.7 4.7 copy.15
  4478.4 2.1 copy.16
  (31 shorter events, 0.4 us)
Async XLA Ops:
  7.2 317.7 %copy-start = (bf16[896,1216]{0,1:T(8,128)(2,1)S(1)}, bf16[896,1216]{0,1:T(8,128)(2,1)}, u32[]{:S(2)}) copy-start(bf16[896,1216]{0,1:T(8,128)(2,1)} %param.9) | copy-start | bytes 6537220
  7.2 262.8 %reduce-scatter.4.cloned.1.call-start = ((), (), s32[]{:S(2)}) async-start(), calls=%async_computation.3 | async-start | bytes 9175040 | tf_op jit(solution)/shard_map/reduce_scatter | solution.py:23
  136.1 7.1 copy-start.5
  143.2 181.7 %all-gather.4.cloned.1.call-start = ((), (), s32[]{:S(2)}) async-start(), calls=%async_computation.4 | async-start | bytes 9175040 | tf_op jit(solution)/shard_map/all_gather | solution.py:29
  275.2 100.8 %all-gather.6.cloned.1.call-start = ((), (), s32[]{:S(2)}) async-start(), calls=%async_computation.6 | async-start | bytes 9175040 | tf_op jit(solution)/shard_map/all_gather | solution.py:37
  275.9 252.4 %reduce-scatter.8.cloned.1.call-start = ((), (), s32[]{:S(2)}) async-start(), calls=%async_computation.7 | async-start | bytes 18350080 | tf_op jit(solution)/shard_map/reduce_scatter | solution.py:43
  401.5 3.7 copy-start.7
  419.7 1.6 copy-start.6
  419.7 219.4 %reduce-scatter.6.cloned.1.call-start = ((), (), s32[]{:S(2)}) async-start(), calls=%async_computation.5 | async-start | bytes 18350080 | tf_op jit(solution)/shard_map/reduce_scatter | solution.py:34
  443.1 85.2 %copy-start.2 = (bf16[1024,896]{1,0:T(8,128)(2,1)S(1)}, bf16[1024,896]{1,0:T(8,128)(2,1)}, u32[]{:S(2)}) copy-start(bf16[1024,896]{1,0:T(8,128)(2,1)} %reduce-scatter.4.cloned.1.call-done) | copy-start | bytes 5505028
  443.1 251.3 %all-gather.8.cloned.1.call-start = ((), (), s32[]{:S(2)}) async-start(), calls=%async_computation.8 | async-start | bytes 9175040 | tf_op jit(solution)/shard_map/all_gather | solution.py:47
  644.8 714.0 %all-reduce.6.cloned.1.call-start = ((), (), s32[]{:S(2)}) async-start(), calls=%async_computation.10 | async-start | bytes 17432576 | tf_op jit(solution)/shard_map/psum | solution.py:50
  679.4 3704.2 %all-reduce.4.cloned.1.call-start = ((), (), s32[]{:S(2)}) async-start(), calls=%async_computation.9 | async-start | bytes 272269312 | tf_op jit(solution)/shard_map/psum | solution.py:49
  704.3 43.4 copy-start.4
  4383.6 96.9 %copy-start.1 = (bf16[896,1216]{0,1:T(8,128)(2,1)S(1)}, bf16[896,1216]{0,1:T(8,128)(2,1)}, u32[]{:S(2)}) copy-start(bf16[896,1216]{0,1:T(8,128)(2,1)} %param.9) | copy-start | bytes 6537220
  4473.7 4.7 copy-start.3
Sparse Core Ops, SparseCore 0:
  143.3 126.6 reduce-scatter.3
  275.3 49.5 all-gather.3
  326.4 49.5 all-gather.5
  419.8 108.4 reduce-scatter.7
  530.7 108.4 reduce-scatter.5
  644.9 49.5 all-gather.7
  697.5 199.5 all-reduce.5
  1358.9 3024.7 all-reduce.3
where the time goes:
time: 4520 us; the launch traced here: 4490 us
  waiting for transfers between devices  3440 us (76%)
  other arithmetic  644 us (14%)
  local copies, waits for them, and re-layouts  272 us (6%)
  matrix products  112 us (2%)
    psum x1, waiting for transfers between devices, per_device(): grad_table = lax.psum(grad_table, 'data')  3020 us
    scatter-add x1, other arithmetic, per_device(): jax.ops.segment_sum(d_embed_all.astype(jnp.float32), jnp.where(is_owned,...  611 us
    reduce_scatter x1, waiting for transfers between devices, per_device(): lax.psum_scatter(partial_rows, 'tensor', scatter_dimension=0, tiled=True)  127 us
    gather x1, local copies, waits for them, and re-layouts, per_device(): picked = jnp.take(embed_table, jnp.where(is_owned, local_ids, 0), axis=0)  127 us
    reduce_scatter x1, waiting for transfers between devices, per_device(): lax.psum_scatter(mlp_part, 'tensor', scatter_dimension=0, tiled=True)  108 us
    unnamed x19, local copies, waits for them, and re-layouts  102 us
  transfers between devices with their start and end apart: 8, of which 7 were waited for; matrix products, arithmetic and copies ran while one was open for 16% of the time, Pallas kernels for 0%

commit v1 on v0

v1 whole, which is shorter than its diff:
```python
import functools

import jax
import jax.numpy as jnp
from jax import lax
from jax.experimental import pallas as pl
from jax.experimental.pallas import tpu as pltpu
from jax.sharding import PartitionSpec as P


NORM_EPS = 1e-6
LOOK_BLOCK = 256
LOOK_GROUP = 32
LOOK_DEPTH = 3
ISSUE = 16
TABLE_BLOCK = 2048
WIDEN_ROWS = 256
LOAD_DEPTH = 3
UNROLL = 8


def gelu_tanh(value):
    return jax.nn.gelu(value, approximate=True)


def lookup_kernel(base, row_ref, count_ref, code_ref, table_ref, out_ref, tiles, sems):
    step, steps = pl.program_id(0), pl.num_programs(0)

    def fetch(block):
        slot = lax.rem(block, LOOK_DEPTH)
        first = (base + block) * LOOK_BLOCK

        def some(j, carry):
            for k in range(ISSUE):
                row = row_ref[first + j * ISSUE + k]

                @pl.when(row >= 0)
                def _():
                    pltpu.make_async_copy(
                        table_ref.at[pl.ds(pl.multiple_of(row, 8), 8), :],
                        tiles.at[slot * LOOK_BLOCK + j * ISSUE + k],
                        sems.at[slot],
                    ).start()

            return carry

        lax.fori_loop(0, LOOK_BLOCK // ISSUE, some, 0)

    @pl.when(step == 0)
    def _():
        def clear(i, carry):
            tiles[pl.ds(i * LOOK_GROUP, LOOK_GROUP)] = jnp.zeros((LOOK_GROUP,) + tiles.shape[1:], tiles.dtype)
            return carry

        lax.fori_loop(0, LOOK_DEPTH * LOOK_BLOCK // LOOK_GROUP, clear, 0)

        def first(slot, carry):
            fetch(slot)
            return carry

        lax.fori_loop(0, jnp.minimum(LOOK_DEPTH - 1, steps), first, 0)

    @pl.when(step + LOOK_DEPTH - 1 < steps)
    def _():
        fetch(step + LOOK_DEPTH - 1)

    slot = lax.rem(step, LOOK_DEPTH)
    count = count_ref[base + step]

    @pl.when(count > 0)
    def _():
        fetched = tiles.at[pl.ds(0, count)]
        pltpu.make_async_copy(fetched, fetched, sems.at[slot]).wait()

    places = lax.broadcasted_iota(jnp.int32, (LOOK_GROUP * 8, LOOK_GROUP), 0)

    for j in range(LOOK_BLOCK // LOOK_GROUP):
        group = pl.ds(j * LOOK_GROUP, LOOK_GROUP)
        pick = (places == code_ref[pl.ds(j, 1), :]).astype(jnp.bfloat16)
        rows = tiles[pl.ds(slot * LOOK_BLOCK + j * LOOK_GROUP, LOOK_GROUP)].reshape(LOOK_GROUP * 8, -1)
        out_ref[group, :] = dot(pick, rows, COLS_BY_COLS).astype(out_ref.dtype)


def lookup_plan(ids, rank, shard_rows):
    local = ids - rank * shard_rows
    owned = (local >= 0) & (local < shard_rows)
    place = lax.broadcasted_iota(jnp.int32, (ids.shape[0] // LOOK_GROUP, LOOK_GROUP), 1) * 8
    code = jnp.where(owned, local & 7, -1 << 20).reshape(place.shape) + place
    row = jnp.where(owned, local & ~7, -1)
    counts = jnp.sum(owned.reshape(-1, LOOK_BLOCK), axis=1).astype(jnp.int32)
    return row, counts, code


def lookup(plan, table, base, count):
    dim = table.shape[1]
    base //= LOOK_BLOCK
    return pl.pallas_call(
        functools.partial(lookup_kernel, base),
        out_shape=jax.ShapeDtypeStruct((count, dim), table.dtype),
        grid_spec=pltpu.PrefetchScalarGridSpec(
            num_scalar_prefetch=2,
            grid=(count // LOOK_BLOCK,),
            in_specs=[
                pl.BlockSpec((LOOK_BLOCK // LOOK_GROUP, LOOK_GROUP), lambda i, r, c: (base + i, 0)),
                pl.BlockSpec(memory_space=pl.ANY),
            ],
            out_specs=pl.BlockSpec((LOOK_BLOCK, dim), lambda i, r, c: (i, 0)),
            scratch_shapes=[
                pltpu.VMEM((LOOK_DEPTH * LOOK_BLOCK, 8, dim), table.dtype),
                pltpu.SemaphoreType.DMA((LOOK_DEPTH,)),
            ],
        ),
        cost_estimate=pl.CostEstimate(flops=count * 5_000_000, bytes_accessed=count * dim * 18, transcendentals=0),
        name="lookup",
    )(*plan, table)


def norm_kernel(kept_ref, got_ref, away_ref, gain_ref, x_ref, normed_ref):
    x = kept_ref[...].astype(jnp.float32) + got_ref[...].astype(jnp.float32) + away_ref[...].astype(jnp.float32)
    x_ref[...] = x.astype(x_ref.dtype)
    inv_rms = lax.rsqrt(jnp.mean(x * x, axis=-1, keepdims=True) + NORM_EPS)
    normed_ref[...] = (x * inv_rms * gain_ref[...]).astype(normed_ref.dtype)


def norm(kept, got, away, gain):
    rows, dim = away.shape
    tile = rows // 2
    here = pl.BlockSpec((tile, dim), lambda i: (i, 0))
    home = pl.BlockSpec((tile, dim), lambda i: (2 + i, 0))
    return pl.pallas_call(
        norm_kernel,
        out_shape=[jax.ShapeDtypeStruct((rows, dim), away.dtype)] * 2,
        grid=(2,),
        in_specs=[home, home, here, pl.BlockSpec((1, dim), lambda i: (0, 0))],
        out_specs=[here, here],
        cost_estimate=pl.CostEstimate(flops=2_000_000_000, bytes_accessed=rows * dim * 10, transcendentals=rows),
        name="norm",
    )(kept, got, away, gain)


def dx_kernel(place_ref, part_ref, got_ref, away_ref, x_ref, grad_ref, gain_ref, dx_ref):
    d_normed = (part_ref[...] + got_ref[...]) + away_ref[...]
    x = x_ref[...].astype(jnp.float32)
    inv_rms = lax.rsqrt(jnp.mean(x * x, axis=-1, keepdims=True) + NORM_EPS)
    x_hat = x * inv_rms
    d_hat = d_normed * gain_ref[...]
    d_norm_in = inv_rms * (d_hat - x_hat * jnp.mean(d_hat * x_hat, axis=-1, keepdims=True))
    dx_ref[...] = (grad_ref[...].astype(jnp.float32) + d_norm_in).astype(dx_ref.dtype)


def norm_grad(place, part, got, away, x, grad, chunk, gain):
    rows, dim = away.shape
    tile = rows // 2
    plain = pl.BlockSpec((tile, dim), lambda i, p: (i, 0))
    return pl.pallas_call(
        dx_kernel,
        out_shape=jax.ShapeDtypeStruct((rows, dim), x.dtype),
        grid_spec=pltpu.PrefetchScalarGridSpec(
            num_scalar_prefetch=1,
            grid=(2,),
            in_specs=[
                pl.BlockSpec((None, None, tile, dim), lambda i, p: (p[0], p[1], i, 0)),
                pl.BlockSpec((None, tile, dim), lambda i, p: (p[0], i, 0)),
                plain,
                plain,
                pl.BlockSpec((tile, dim), lambda i, p: (2 * chunk + i, 0)),
                pl.BlockSpec((1, dim), lambda i, p: (0, 0)),
            ],
            out_specs=plain,
        ),
        cost_estimate=pl.CostEstimate(flops=3_000_000_000, bytes_accessed=rows * dim * 18, transcendentals=rows),
        name="norm_grad",
    )(place, part, got, away, x, grad, gain)


def table_kernel(start_ref, key_ref, flip_ref, *refs):
    *dx_refs, table_ref, rows_f32, stage, sums_f32, sems, out_sems = refs
    block, blocks = pl.program_id(0), pl.num_programs(0)
    part, dim = dx_refs[0].shape
    tokens = len(dx_refs) * part

    @pl.when(block == 0)
    def _():
        def load(i):
            return pltpu.make_async_copy(dx_refs[i], stage.at[i % LOAD_DEPTH], sems.at[i % LOAD_DEPTH])

        for i in range(LOAD_DEPTH - 1):
            load(i).start()
        for i in range(len(dx_refs)):
            if i + LOAD_DEPTH - 1 < len(dx_refs):
                load(i + LOAD_DEPTH - 1).start()
            load(i).wait()

            def widen(j, carry, i=i):
                rows = pl.ds(pl.multiple_of(j * WIDEN_ROWS, WIDEN_ROWS), WIDEN_ROWS)
                wide = pl.ds(pl.multiple_of(i * part + j * WIDEN_ROWS, WIDEN_ROWS), WIDEN_ROWS)
                rows_f32[wide, :] = stage[i % LOAD_DEPTH, rows, :].astype(jnp.float32)
                return carry

            lax.fori_loop(0, part // WIDEN_ROWS, widen, 0)

    slot = lax.rem(block, 2)
    whole, rest = table_ref.shape[0] // TABLE_BLOCK, table_ref.shape[0] % TABLE_BLOCK

    def put(i, rows):
        at = lax.rem(i, 2)
        return pltpu.make_async_copy(
            sums_f32.at[at, pl.ds(0, rows), :],
            table_ref.at[pl.ds(pl.multiple_of(i * TABLE_BLOCK, TABLE_BLOCK), rows), :],
            out_sems.at[at],
        )

    @pl.when(block >= 2)
    def _():
        put(block - 2, TABLE_BLOCK).wait()

    def clear(i, carry):
        sums_f32[slot, pl.ds(pl.multiple_of(i * 128, 128), 128), :] = jnp.zeros((128, dim), jnp.float32)
        return carry

    lax.fori_loop(0, TABLE_BLOCK // 128, clear, 0)
    first, last, flip = start_ref[block], start_ref[block + 1], flip_ref[0]

    def add(k, carry):
        previous, total = carry
        key = key_ref[k]
        row = (key // tokens) & (TABLE_BLOCK - 1)
        value = rows_f32[pl.ds((key & (tokens - 1)) ^ flip, 1), :]
        return row, jnp.where(row == previous, total + value, value)

    def group(g, carry):
        sums = []
        for u in range(UNROLL):
            carry = add(first + g * UNROLL + u, carry)
            sums.append(carry)
        for row, total in sums:
            sums_f32[slot, pl.ds(row, 1), :] = total
        return carry

    def single(k, carry):
        carry = add(k, carry)
        sums_f32[slot, pl.ds(carry[0], 1), :] = carry[1]
        return carry

    carry = (jnp.int32(-1), jnp.zeros((1, dim), jnp.float32))
    groups = (last - first) // UNROLL
    carry = lax.fori_loop(0, groups, group, carry)
    lax.fori_loop(first + groups * UNROLL, last, single, carry)

    @pl.when(block < whole)
    def _():
        put(block, TABLE_BLOCK).start()

    @pl.when(block == blocks - 1)
    def _():
        if rest:
            put(block, rest).start()
        if table_ref.shape[0] > TABLE_BLOCK:
            put(block - 1, TABLE_BLOCK).wait()
        put(block, rest or TABLE_BLOCK).wait()


def table_plan(ids, rank, shard_rows):
    tokens = ids.shape[0]
    local = ids - rank * shard_rows
    owned = (local >= 0) & (local < shard_rows)
    blocks = pl.cdiv(shard_rows, TABLE_BLOCK)
    key = jnp.where(owned, local, shard_rows + TABLE_BLOCK) * tokens + jnp.arange(tokens, dtype=jnp.int32)
    key = lax.sort(key)
    bounds = jnp.minimum(jnp.arange(blocks + 1, dtype=jnp.int32) * TABLE_BLOCK, shard_rows) * tokens
    return jnp.sum((key[None, :] < bounds[:, None]).astype(jnp.int32), axis=1), key


def table_grad(start, key, flip, dx_parts, shard_rows):
    part, dim = dx_parts[0].shape
    return pl.pallas_call(
        table_kernel,
        out_shape=jax.ShapeDtypeStruct((shard_rows, dim), jnp.float32),
        grid_spec=pltpu.PrefetchScalarGridSpec(
            num_scalar_prefetch=3,
            grid=(start.shape[0] - 1,),
            in_specs=[pl.BlockSpec(memory_space=pl.ANY)] * len(dx_parts),
            out_specs=pl.BlockSpec(memory_space=pl.ANY),
            scratch_shapes=[
                pltpu.VMEM((len(dx_parts) * part + 8, dim), jnp.float32),
                pltpu.VMEM((LOAD_DEPTH, part, dim), jnp.bfloat16),
                pltpu.VMEM((2, TABLE_BLOCK + 8, dim), jnp.float32),
                pltpu.SemaphoreType.DMA((LOAD_DEPTH,)),
                pltpu.SemaphoreType.DMA((2,)),
            ],
        ),
        compiler_params=pltpu.CompilerParams(vmem_limit_bytes=58 << 20),
        cost_estimate=pl.CostEstimate(flops=60_000_000_000, bytes_accessed=shard_rows * dim * 4, transcendentals=0),
        name="table_grad",
    )(start, key, flip, *dx_parts)


CORE_SWAP = [(0, 1), (1, 0), (2, 3), (3, 2)]
CHIP_SWAP = [(0, 2), (2, 0), (1, 3), (3, 1)]
DATA_SWAP = [(0, 1), (1, 0)]
ROWS_BY_COLS = (((1,), (0,)), ((), ()))
ROWS_BY_ROWS = (((1,), (1,)), ((), ()))
COLS_BY_COLS = (((0,), (0,)), ((), ()))


def dot(a, b, dims):
    return lax.dot_general(a, b, dims, preferred_element_type=jnp.float32)


def after(value, *others):
    return lax.optimization_barrier((value,) + others)[0]


def solution(mesh):
    tok_spec = P(("pod", "data", "tensor"), None)

    def per_device(token_ids, embed_table, norm_gain, w_in, w_out, d_out):
        shard_rows, dim = embed_table.shape
        tok_dev = d_out.shape[0]
        part = tok_dev // 2
        rank, replica = lax.axis_index("tensor"), lax.axis_index("data")
        chip, core = rank // 2, rank % 2
        gain_f32 = norm_gain.astype(jnp.float32)[None]
        place = jnp.stack([chip, core]).astype(jnp.int32)
        places = token_ids.reshape(2, 2, 2, part)
        places = jnp.where(chip == 0, places[::-1], places)
        places = jnp.where(core == 0, places[:, ::-1], places)
        look = lookup_plan(places.transpose(2, 1, 0, 3).reshape(-1), rank, shard_rows)

        def gather(value):
            return lax.all_gather(value, "tensor", axis=0, tiled=True)

        ids_other = lax.ppermute(token_ids, "data", DATA_SWAP)
        ids_low, ids_high = jnp.where(replica == 0, token_ids, ids_other), jnp.where(replica == 0, ids_other, token_ids)
        ids_all = jnp.stack([ids_low, ids_high]).reshape(2, 4, 2, part).transpose(2, 1, 0, 3).reshape(-1)
        start, key = table_plan(ids_all, rank, shard_rows)
        flip = ((rank * 2 + replica) * part).astype(jnp.int32)[None]

        grad_gathered = lax.all_gather(d_out.reshape(2, part, dim), "tensor", axis=1, tiled=True)
        grad_all = [grad_gathered[0], grad_gathered[1]]

        looked, aways = [], []
        for c in range(2):
            sent = lookup(look, embed_table, 4 * c * part, 2 * part)
            got = lax.ppermute(sent, "tensor", CORE_SWAP)
            kept = lookup(look, embed_table, (4 * c + 2) * part, 2 * part)
            looked.append((kept, got))
            aways.append(lax.ppermute(kept[:part] + got[:part], "tensor", CHIP_SWAP))

        embedded, normed_all = [], []
        for c in range(2):
            x, normed = norm(*looked[c], aways[c], gain_f32)
            embedded.append(x)
            normed_all.append(gather(after(normed, grad_gathered)))
        normed_all[0] = after(normed_all[0], key)

        def core_sum(value):
            value = value.reshape(2, 2, part, dim)
            send = lax.dynamic_index_in_dim(value, 1 - core, 1, keepdims=False)
            return value, lax.ppermute(send, "tensor", CORE_SWAP)

        def chip_sum(value, got, wait_for=None):
            mine = lax.dynamic_slice(value, (1 - chip, core, 0, 0), (1, 1, part, dim)).reshape(part, dim)
            away = mine + lax.dynamic_index_in_dim(got, 1 - chip, 0, keepdims=False)
            away = away if wait_for is None else after(away, wait_for)
            return value, got, lax.ppermute(away, "tensor", CHIP_SWAP)

        def up(c):
            return dot(normed_all[c], w_in, ROWS_BY_COLS).astype(jnp.bfloat16)

        def down(c, pre_gelu):
            gelu_pull = jax.vjp(gelu_tanh, pre_gelu.astype(jnp.float32))[1]
            grad_hidden = dot(grad_all[c], w_out, ROWS_BY_ROWS)
            grad_pre = gelu_pull(grad_hidden)[0].astype(jnp.bfloat16)
            norm_part = dot(grad_pre, w_in, ROWS_BY_ROWS)
            return grad_pre, norm_part, core_sum(norm_part)

        def act(pre_gelu):
            return gelu_tanh(pre_gelu.astype(jnp.float32)).astype(jnp.bfloat16)

        pre_0 = up(0)
        grad_pre_0, norm_part_0, d_normed_0 = down(0, pre_0)
        normed_all[1] = after(normed_all[1], norm_part_0)
        pre_1 = up(1)
        hidden = [act(pre_0), act(pre_1)]
        grad_w_out = dot(hidden[0], grad_all[0], COLS_BY_COLS) + dot(hidden[1], grad_all[1], COLS_BY_COLS)
        cut = grad_w_out.shape[0] // 2
        other_out_0 = lax.ppermute(grad_w_out[:cut], "data", DATA_SWAP)
        grad_pre_1, _, d_normed_1 = down(1, after(pre_1, grad_w_out))

        def to_dx(c, sums):
            return norm_grad(place, *sums, embedded[c], d_out, c, gain_f32)

        dx_0 = to_dx(0, chip_sum(*d_normed_0))
        crossed_0 = lax.ppermute(dx_0, "data", DATA_SWAP)
        other_out_1 = lax.ppermute(after(grad_w_out[cut:], dx_0), "data", DATA_SWAP)

        grad_pre = [after(g, dx_0) for g in (grad_pre_0, grad_pre_1)]
        grad_w_in = dot(normed_all[0], grad_pre[0], COLS_BY_COLS) + dot(normed_all[1], grad_pre[1], COLS_BY_COLS)

        y_sums = []
        for c in range(2):
            mlp_part = dot(hidden[c], w_out, ROWS_BY_COLS)
            y_sums.append(core_sum(mlp_part))

        dx_1 = to_dx(1, chip_sum(*d_normed_1))
        crossed_1 = lax.ppermute(dx_1, "data", DATA_SWAP)
        other_in = lax.ppermute(after(grad_w_in, dx_1), "data", DATA_SWAP)

        dx_all = []
        for dx, crossed in ((dx_0, crossed_0), (dx_1, crossed_1)):
            pair = jnp.concatenate([dx, crossed])
            from_core = lax.ppermute(pair, "tensor", CORE_SWAP)
            from_chip = lax.ppermute(pair, "tensor", CHIP_SWAP)
            from_both = lax.ppermute(from_chip, "tensor", CORE_SWAP)
            dx_all += [pair, from_core, from_chip, from_both]
        y_1 = chip_sum(*y_sums[1], wait_for=from_chip)
        y_0 = chip_sum(*y_sums[0], wait_for=from_chip)
        y_sums = [y_0, y_1]
        grad_table = table_grad(start, key, flip, dx_all, shard_rows)

        block_out = []
        for c, (value, got, away) in enumerate(y_sums):
            mine = lax.dynamic_slice(value, (chip, core, 0, 0), (1, 1, part, dim)).reshape(part, dim)
            mlp_out = (mine + lax.dynamic_index_in_dim(got, chip, 0, keepdims=False)) + after(away, grad_table)
            block_out.append((embedded[c].astype(jnp.float32) + mlp_out).astype(jnp.bfloat16))
        block_out = jnp.concatenate(block_out)
        grad_w_in = grad_w_in + after(other_in, grad_table)
        grad_w_out = grad_w_out + jnp.concatenate([other_out_0, after(other_out_1, grad_table)])
        return block_out, grad_table, grad_w_in, grad_w_out

    return jax.shard_map(
        per_device,
        mesh=mesh,
        in_specs=(P(("pod", "data")), P("tensor", None), P(None), P(None, "tensor"), P("tensor", None), tok_spec),
        out_specs=(tok_spec, P(("pod", "tensor"), None), P("pod", "tensor"), P(("pod", "tensor"), None)),
        check_vma=False,
    )
```

time: 4520 us -> 607 us (0.13)
  waiting for transfers between devices: 3440 us -> 264 us
  other arithmetic: 644 us -> 47.7 us
  local copies, waits for them, and re-layouts: 272 us -> 27.5 us
  Pallas kernels: 0 us -> 124 us
    psum x2 -> x0, waiting for transfers between devices: 3020 us -> none  [the longest x1 3020 us: per_device(): grad_table = lax.psum(grad_table, 'data')]
    scatter-add x1 -> x0, other arithmetic: 611 us -> none  [per_device(): jax.ops.segment_sum(d_embed_all.astype(jnp.float32), jnp.where(is_owned,...]
    reduce_scatter x3 -> x0, waiting for transfers between devices: 320 us -> none  [the longest x1 127 us: per_device(): lax.psum_scatter(partial_rows, 'tensor', scatter_dimension=0, tiled=True)]
    ppermute x0 -> x24, waiting for transfers between devices: none -> 260 us  [the longest x1 68.9 us: per_device(): other_in = lax.ppermute(after(grad_w_in, dx_1), 'data', DATA_SWAP)]
    gather x1 -> x0, local copies, waits for them, and re-layouts: 127 us -> none  [per_device(): picked = jnp.take(embed_table, jnp.where(is_owned, local_ids, 0), axis=0)]
    pallas_call x0 -> x9, Pallas kernels: none -> 124 us  [the longest x1 70.5 us: table_grad(): pl.pallas_call(table_kernel, out_shape=jax.ShapeDtypeStruct((shard_rows,...]
    all_gather x3, waiting for transfers between devices: 99 us -> 2.51 us  [the longest x1 2.5 us: per_device(): lax.all_gather(d_out.reshape(2, part, dim), 'tensor', axis=1, tiled=True)]
    unnamed x19 -> x78, local copies, waits for them, and re-layouts: 102 us -> 13.1 us
  transfers between devices with their start and end apart: 8 -> 27, of which waited for: 7 -> 10; matrix products, arithmetic and copies ran while one was open for 16% -> 27% of each run, Pallas kernels for 0% -> 21%
where the time goes in v1:
time: 607 us; the launch traced here: 598 us
  waiting for transfers between devices  264 us (43%)
  Pallas kernels  124 us (20%)
  matrix products  103 us (17%)
  other arithmetic  47.7 us (8%)
  local copies, waits for them, and re-layouts  27.5 us (5%)
  starting transfers between devices  18.1 us (3%)
  between operations  14.6 us (2%)
    dot_general x12, matrix products, dot(): return lax.dot_general(a, b, dims, preferred_element_type=jnp.float32)  103 us
    pallas_call x1, Pallas kernels, table_grad(): pl.pallas_call(table_kernel, out_shape=jax.ShapeDtypeStruct((shard_rows,...  70.5 us
    ppermute x1, waiting for transfers between devices, per_device(): other_in = lax.ppermute(after(grad_w_in, dx_1), 'data', DATA_SWAP)  68.9 us
    ppermute x2, waiting for transfers between devices, per_device(): aways.append(lax.ppermute(kept[:part] + got[:part], 'tensor', CHIP_SWAP))  68.2 us
    ppermute x4, waiting for transfers between devices, chip_sum(): return (value, got, lax.ppermute(away, 'tensor', CHIP_SWAP))  56.2 us
    ppermute x2, waiting for transfers between devices, per_device(): from_chip = lax.ppermute(pair, 'tensor', CHIP_SWAP)  46.3 us
    pallas_call x4, Pallas kernels, lookup(): pl.pallas_call(functools.partial(lookup_kernel, base), out_shape=jax.Shap...  37.3 us
    ppermute x1, waiting for transfers between devices, per_device(): crossed_1 = lax.ppermute(dx_1, 'data', DATA_SWAP)  18.4 us
  transfers between devices with their start and end apart: 27, of which 10 were waited for; matrix products, arithmetic and copies ran while one was open for 27% of the time, Pallas kernels for 21%

profile of v1, /device:TPU:0, one launch (start us, length us, event | category | flops | bytes accessed | tf_op | source)
XLA Modules:
  0.0 598.4 jit_solution(17909892266755651127)
XLA Ops:
  10.9 9.3 %lookup.5 = bf16[1024,896]{1,0:T(8,128)(2,1)} custom-call(s32[4096]{0:T(1024)} %bitcast.107, s32[16]{0:T(128)} %reduce_sum.18.count_ref, s32[128,32]{1,0:T(8,128)} %broadcast_add_fusion.code_ref, bf16[37984,896]{1,0:T(8,128)(2,1)} %table_ref.7), custom_call_target="tpu_custom_call" | custom-call | flops 5120000000 | bytes 16515072 | tf_op jit(solution)/shard_map/lookup/pallas_call | solution.py:97
  21.0 9.3 %lookup.4.kept_ref = bf16[1024,896]{1,0:T(8,128)(2,1)} custom-call(s32[4096]{0:T(1024)} %bitcast.108, s32[16]{0:T(128)} %reduce_sum.18.count_ref, s32[128,32]{1,0:T(8,128)} %broadcast_add_fusion.code_ref, bf16[37984,896]{1,0:T(8,128)(2,1)} %table_ref.7), custom_call_target="tpu_custom_call" | custom-call | flops 5120000000 | bytes 16515072 | tf_op jit(solution)/shard_map/lookup/pallas_call | solution.py:97
  35.0 40.2 %collective-permute-done.1.away_ref = bf16[512,896]{1,0:T(8,128)(2,1)S(1)} collective-permute-done((bf16[512,896]{1,0:T(8,128)(2,1)S(1)}, bf16[512,896]{1,0:T(8,128)(2,1)S(1)}, u32[]{:S(2)}, u32[]{:S(2)}) %collective-permute-start.1) | collective-permute-done | bytes 917536 | tf_op jit(solution)/shard_map/ppermute | solution.py:348
  81.6 9.4 %lookup.7 = bf16[1024,896]{1,0:T(8,128)(2,1)} custom-call(s32[4096]{0:T(1024)} %bitcast.109, s32[16]{0:T(128)} %reduce_sum.18.count_ref, s32[128,32]{1,0:T(8,128)} %broadcast_add_fusion.code_ref, bf16[37984,896]{1,0:T(8,128)(2,1)} %table_ref.7), custom_call_target="tpu_custom_call" | custom-call | flops 5120000000 | bytes 16515072 | tf_op jit(solution)/shard_map/lookup/pallas_call | solution.py:97
  91.2 9.3 %lookup.6.kept_ref = bf16[1024,896]{1,0:T(8,128)(2,1)} custom-call(s32[4096]{0:T(1024)} %bitcast.110, s32[16]{0:T(128)} %reduce_sum.18.count_ref, s32[128,32]{1,0:T(8,128)} %broadcast_add_fusion.code_ref, bf16[37984,896]{1,0:T(8,128)(2,1)} %table_ref.7), custom_call_target="tpu_custom_call" | custom-call | flops 5120000000 | bytes 16515072 | tf_op jit(solution)/shard_map/lookup/pallas_call | solution.py:97
  102.5 28.0 %collective-permute-done.5.away_ref = bf16[512,896]{1,0:T(8,128)(2,1)S(1)} collective-permute-done((bf16[512,896]{1,0:T(8,128)(2,1)S(1)}, bf16[512,896]{1,0:T(8,128)(2,1)S(1)}, u32[]{:S(2)}, u32[]{:S(2)}) %collective-permute-start.5) | collective-permute-done | bytes 917536 | tf_op jit(solution)/shard_map/ppermute | solution.py:348
  138.2 6.8 %sort.10 = (s32[8192]{0:T(1024)}, s32[8192]{0:T(1024)}) sort(s32[8192]{0:T(1024)S(1)} %iota_add_fusion, s32[8192]{0:T(1024)S(1)} %iota.20), dimensions={0}, to_apply=%region_1.2 | sort | flops 106496 | bytes 131072 | tf_op jit(solution)/shard_map/sort | solution.py:269
  145.0 7.8 %convolution_convert_fusion.1 = bf16[2048,1216]{0,1:T(8,128)(2,1)S(1)} fusion(bf16[2048,896]{1,0:T(8,128)(2,1)} %all-gather.6.cloned.1.call-done, bf16[896,1216]{0,1:T(8,128)(2,1)S(1)} %copy-done), kind=kOutput, calls=%fused_computation.39 | convolution fusion | flops 4465229824 | bytes 10829824 | tf_op jit(solution)/shard_map/dot_general | solution.py:307
  152.8 14.1 %fusion.4 = bf16[2048,1216]{0,1:T(8,128)(2,1)S(1)} fusion(bf16[2048,1216]{0,1:T(8,128)(2,1)S(1)} %convolution_convert_fusion.1, bf16[1216,896]{1,0:T(8,128)(2,1)S(1)} %copy-done.16, bf16[2,2048,896]{2,1,0:T(8,128)(2,1)} %all-gather.4.cloned.1.call-done), kind=kOutput, calls=%fused_computation.17 | convolution fusion | flops 4515037184 | bytes 15810560 | tf_op jit(solution)/shard_map/dot_general | solution.py:307
  166.9 5.8 fusion.43
  177.9 8.0 %convolution_convert_fusion = bf16[2048,1216]{0,1:T(8,128)(2,1)S(1)} fusion(bf16[2048,896]{1,0:T(8,128)(2,1)} %all-gather.8.cloned.1.call-done, bf16[896,1216]{0,1:T(8,128)(2,1)S(1)} %copy-done), kind=kOutput, calls=%fused_computation.38 | convolution fusion | flops 4465229824 | bytes 10829824 | tf_op jit(solution)/shard_map/dot_general | solution.py:307
  185.9 10.9 %fusion.26 = f32[1216,896]{1,0:T(8,128)S(1)} fusion(bf16[2,2048,896]{2,1,0:T(8,128)(2,1)} %all-gather.4.cloned.1.call-done, bf16[2048,1216]{0,1:T(8,128)(2,1)} %copy-done.29), kind=kOutput, calls=%fused_computation.50 | convolution fusion | flops 4487643136 | bytes 13008896 | tf_op jit(solution)/shard_map/dot_general | solution.py:307
  196.9 7.9 %convolution_add_fusion.1 = f32[1216,896]{1,0:T(8,128)} fusion(f32[1216,896]{1,0:T(8,128)S(1)} %fusion.26, bf16[2,2048,896]{2,1,0:T(8,128)(2,1)S(1)} %bitcast.115, bf16[2048,1216]{0,1:T(8,128)(2,1)S(1)} %convolution_convert_fusion), kind=kOutput, calls=%fused_computation.42 | convolution fusion | flops 4488732672 | bytes 17367040 | tf_op jit(solution)/shard_map/dot_general | solution.py:307
  204.8 12.0 %fusion.7 = bf16[2048,1216]{0,1:T(8,128)(2,1)S(1)} fusion(bf16[2048,1216]{0,1:T(8,128)(2,1)S(1)} %convolution_convert_fusion, bf16[1216,896]{1,0:T(8,128)(2,1)S(1)} %copy-done.17, bf16[2,2048,896]{2,1,0:T(8,128)(2,1)S(1)} %bitcast.115), kind=kOutput, calls=%fused_computation.20 | convolution fusion | flops 4515037184 | bytes 15810560 | tf_op jit(solution)/shard_map/dot_general | solution.py:307
  216.9 5.8 fusion.44
  228.5 8.7 %fusion.37 = f32[2048,896]{1,0:T(8,128)S(1)} fusion(bf16[1216,896]{1,0:T(8,128)(2,1)S(1)} %copy-done.18, bf16[2048,1216]{0,1:T(8,128)(2,1)} %copy-done.29), kind=kOutput, calls=%fused_computation.86 | convolution fusion | flops 4487643136 | bytes 14499840 | tf_op jit(solution)/shard_map/dot_general | solution.py:307
  239.4 5.3 bitcast_add_fusion.2
  250.2 7.6 %fusion.39 = f32[2048,896]{1,0:T(8,128)S(1)} fusion(bf16[1216,896]{1,0:T(8,128)(2,1)S(1)} %copy-done.19, bf16[2048,1216]{0,1:T(8,128)(2,1)S(1)} %bitcast.119), kind=kOutput, calls=%fused_computation.87 | convolution fusion | flops 4487643136 | bytes 14499840 | tf_op jit(solution)/shard_map/dot_general | solution.py:307
  263.6 24.1 %collective-permute-done.12.away_ref = f32[512,896]{1,0:T(8,128)} collective-permute-done((f32[512,896]{1,0:T(8,128)S(1)}, f32[512,896]{1,0:T(8,128)}, u32[]{:S(2)}, u32[]{:S(2)}) %collective-permute-start.12) | collective-permute-done | bytes 1835040 | tf_op jit(solution)/shard_map/ppermute | solution.py:366
  287.7 5.0 norm_grad.3
  294.1 32.1 %collective-permute-done.7.away_ref = f32[512,896]{1,0:T(8,128)S(1)} collective-permute-done((f32[512,896]{1,0:T(8,128)}, f32[512,896]{1,0:T(8,128)S(1)}, u32[]{:S(2)}, u32[]{:S(2)}) %collective-permute-start.7) | collective-permute-done | bytes 1835040 | tf_op jit(solution)/shard_map/ppermute | solution.py:366
  327.4 5.1 norm_grad.2
  336.0 18.4 %collective-permute-done.8 = bf16[512,896]{1,0:T(8,128)(2,1)S(1)} collective-permute-done((bf16[512,896]{1,0:T(8,128)(2,1)}, bf16[512,896]{1,0:T(8,128)(2,1)S(1)}, u32[]{:S(2)}, u32[]{:S(2)}) %collective-permute-start.8) | collective-permute-done | bytes 917536 | tf_op jit(solution)/shard_map/ppermute | solution.py:407
  357.0 4.7 fusion.42
  369.8 8.8 %collective-permute-done.15.refs_2_ = bf16[1024,896]{1,0:T(8,128)(2,1)} collective-permute-done((bf16[1024,896]{1,0:T(8,128)(2,1)}, bf16[1024,896]{1,0:T(8,128)(2,1)}, u32[]{:S(2)}, u32[]{:S(2)}) %collective-permute-start.15) | collective-permute-done | bytes 1835040 | tf_op jit(solution)/shard_map/ppermute | solution.py:414
  378.6 37.5 %collective-permute-done.9.refs_6_ = bf16[1024,896]{1,0:T(8,128)(2,1)} collective-permute-done((bf16[1024,896]{1,0:T(8,128)(2,1)S(1)}, bf16[1024,896]{1,0:T(8,128)(2,1)}, u32[]{:S(2)}, u32[]{:S(2)}) %collective-permute-start.9) | collective-permute-done | bytes 1835040 | tf_op jit(solution)/shard_map/ppermute | solution.py:414
  416.1 7.2 %fusion.45 = f32[896,1216]{0,1:T(8,128)S(1)} fusion(bf16[2048,1216]{0,1:T(8,128)(2,1)} %copy-done.27, bf16[2048,896]{1,0:T(8,128)(2,1)S(1)} %copy-done.15), kind=kOutput, calls=%fused_computation.91 | convolution fusion | flops 4462739456 | bytes 13008896 | tf_op jit(solution)/shard_map/dot_general | solution.py:307
  423.3 7.1 %convolution_add_fusion = f32[896,1216]{0,1:T(8,128)} fusion(f32[896,1216]{0,1:T(8,128)S(1)} %fusion.45, bf16[2048,1216]{0,1:T(8,128)(2,1)S(1)} %bitcast.117, bf16[2048,896]{1,0:T(8,128)(2,1)S(1)} %copy-done.14), kind=kOutput, calls=%fused_computation.41 | convolution fusion | flops 4463828992 | bytes 17367040 | tf_op jit(solution)/shard_map/dot_general | solution.py:307
  434.5 70.5 %table_grad.1 = f32[37984,896]{1,0:T(8,128)} custom-call(s32[20]{0:T(128)} %convert_reduce_fusion.start_ref, s32[8192]{0:T(1024)} %get-tuple-element.28.key_ref, s32[1]{0:T(128)} %bitcast.19.flip_ref, bf16[1024,896]{1,0:T(8,128)(2,1)} %pad_maximum_fusion.1.refs_0_, bf16[1024,896]{1,0:T(8,128)(2,1)} %copy-done.20, ...), custom_call_target="tpu_custom_call" | custom-call | flops 60000002048 | bytes 136134656 | tf_op jit(solution)/shard_map/table_grad/pallas_call | solution.py:276
  505.1 68.9 %collective-permute-done.21 = f32[896,1216]{0,1:T(8,128)} collective-permute-done((f32[896,1216]{0,1:T(8,128)}, f32[896,1216]{0,1:T(8,128)}, u32[]{:S(2)}, u32[]{:S(2)}) %collective-permute-start.21) | collective-permute-done | bytes 4358176 | tf_op jit(solution)/shard_map/ppermute | solution.py:408
  573.9 6.1 %add.146 = f32[896,1216]{0,1:T(8,128)} add(f32[896,1216]{0,1:T(8,128)} %convolution_add_fusion, f32[896,1216]{0,1:T(8,128)} %collective-permute-done.21) | non-fusion elementwise | flops 1089536 | bytes 13074432 | tf_op jit(solution)/shard_map/add | solution.py:428
  587.5 4.1 maximum_add_fusion
  (170 shorter events, 77.6 us)
Async XLA Ops:
  7.2 137.8 %copy-start = (bf16[896,1216]{0,1:T(8,128)(2,1)S(1)}, bf16[896,1216]{0,1:T(8,128)(2,1)}, u32[]{:S(2)}) copy-start(bf16[896,1216]{0,1:T(8,128)(2,1)} %param.9) | copy-start | bytes 6537220
  7.2 74.4 %all-gather.4.cloned.1.call-start = ((), (), s32[]{:S(2)}) async-start(), calls=%async_computation | async-start | bytes 9175040 | tf_op jit(solution)/shard_map/all_gather | solution.py:339
  7.9 137.0 %all-gather.6.cloned.1.call-start = ((), (), s32[]{:S(2)}) async-start(), calls=%async_computation.1 | async-start | bytes 4587520 | tf_op jit(solution)/shard_map/all_gather | solution.py:331
  20.2 10.1 %collective-permute-start = (bf16[1024,896]{1,0:T(8,128)(2,1)}, bf16[1024,896]{1,0:T(8,128)(2,1)}, u32[]{:S(2)}, u32[]{:S(2)}) collective-permute-start(bf16[1024,896]{1,0:T(8,128)(2,1)} %lookup.5), channel_id=1, source_target_pairs={{0,1},{1,0},{2,3},{3,2},{4,5},{5,4},{6,7},{7,6}} | collective-permute-start | bytes 5505032 | tf_op jit(solution)/shard_map/ppermute | solution.py:345
  31.9 43.3 %collective-permute-start.1 = (bf16[512,896]{1,0:T(8,128)(2,1)S(1)}, bf16[512,896]{1,0:T(8,128)(2,1)S(1)}, u32[]{:S(2)}, u32[]{:S(2)}) collective-permute-start(bf16[512,896]{1,0:T(8,128)(2,1)S(1)} %slice_add_fusion.1), channel_id=1, source_target_pairs={{0,2},{2,0},{1,3},{3,1},{4,6},{6,4},{5,7},{7,5}} | collective-permute-start | bytes 2752520 | tf_op jit(solution)/shard_map/ppermute | solution.py:348
  81.6 96.3 %all-gather.8.cloned.1.call-start = ((), (), s32[]{:S(2)}) async-start(), calls=%async_computation.2 | async-start | bytes 4587520 | tf_op jit(solution)/shard_map/all_gather | solution.py:331
  91.0 9.6 %collective-permute-start.4 = (bf16[1024,896]{1,0:T(8,128)(2,1)}, bf16[1024,896]{1,0:T(8,128)(2,1)}, u32[]{:S(2)}, u32[]{:S(2)}) collective-permute-start(bf16[1024,896]{1,0:T(8,128)(2,1)} %lookup.7), channel_id=1, source_target_pairs={{0,1},{1,0},{2,3},{3,2},{4,5},{5,4},{6,7},{7,6}} | collective-permute-start | bytes 5505032 | tf_op jit(solution)/shard_map/ppermute | solution.py:345
  102.1 28.3 %collective-permute-start.5 = (bf16[512,896]{1,0:T(8,128)(2,1)S(1)}, bf16[512,896]{1,0:T(8,128)(2,1)S(1)}, u32[]{:S(2)}, u32[]{:S(2)}) collective-permute-start(bf16[512,896]{1,0:T(8,128)(2,1)S(1)} %slice_add_fusion), channel_id=1, source_target_pairs={{0,2},{2,0},{1,3},{3,1},{4,6},{6,4},{5,7},{7,5}} | collective-permute-start | bytes 2752520 | tf_op jit(solution)/shard_map/ppermute | solution.py:348
  134.3 3.8 collective-permute-start.2
  177.9 61.5 %collective-permute-start.11 = (f32[2,512,896]{2,1,0:T(8,128)}, f32[2,512,896]{2,1,0:T(8,128)}, u32[]{:S(2)}, u32[]{:S(2)}) collective-permute-start(f32[2,512,896]{2,1,0:T(8,128)} %dynamic-slice_bitcast_fusion.1), channel_id=1, source_target_pairs={{0,1},{1,0},{2,3},{3,2},{4,5},{5,4},{6,7},{7,6}} | collective-permute-start | bytes 11010056 | tf_op jit(solution)/shard_map/ppermute | solution.py:360
  228.0 17.1 %collective-permute-start.6 = (f32[2,512,896]{2,1,0:T(8,128)}, f32[2,512,896]{2,1,0:T(8,128)}, u32[]{:S(2)}, u32[]{:S(2)}) collective-permute-start(f32[2,512,896]{2,1,0:T(8,128)} %dynamic-slice_bitcast_fusion.2), channel_id=1, source_target_pairs={{0,1},{1,0},{2,3},{3,2},{4,5},{5,4},{6,7},{7,6}} | collective-permute-start | bytes 11010056 | tf_op jit(solution)/shard_map/ppermute | solution.py:360
  239.3 124.0 %collective-permute-start.3 = (f32[2,512,896]{2,1,0:T(8,128)}, f32[2,512,896]{2,1,0:T(8,128)}, u32[]{:S(2)}, u32[]{:S(2)}) collective-permute-start(f32[2,512,896]{2,1,0:T(8,128)} %dynamic-slice_bitcast_fusion.3), channel_id=1, source_target_pairs={{0,1},{1,0},{2,3},{3,2},{4,5},{5,4},{6,7},{7,6}} | collective-permute-start | bytes 11010056 | tf_op jit(solution)/shard_map/ppermute | solution.py:360
  244.7 43.0 %collective-permute-start.12 = (f32[512,896]{1,0:T(8,128)S(1)}, f32[512,896]{1,0:T(8,128)}, u32[]{:S(2)}, u32[]{:S(2)}) collective-permute-start(f32[512,896]{1,0:T(8,128)S(1)} %bitcast_add_fusion.2), channel_id=1, source_target_pairs={{0,2},{2,0},{1,3},{3,1},{4,6},{6,4},{5,7},{7,5}} | collective-permute-start | bytes 5505032 | tf_op jit(solution)/shard_map/ppermute | solution.py:366
  248.5 77.7 %collective-permute-start.7 = (f32[512,896]{1,0:T(8,128)}, f32[512,896]{1,0:T(8,128)S(1)}, u32[]{:S(2)}, u32[]{:S(2)}) collective-permute-start(f32[512,896]{1,0:T(8,128)} %bitcast_add_fusion.3), channel_id=1, source_target_pairs={{0,2},{2,0},{1,3},{3,1},{4,6},{6,4},{5,7},{7,5}} | collective-permute-start | bytes 5505032 | tf_op jit(solution)/shard_map/ppermute | solution.py:366
  262.9 102.7 %collective-permute-start.19 = (f32[2,512,896]{2,1,0:T(8,128)}, f32[2,512,896]{2,1,0:T(8,128)}, u32[]{:S(2)}, u32[]{:S(2)}) collective-permute-start(f32[2,512,896]{2,1,0:T(8,128)} %dynamic-slice_bitcast_fusion), channel_id=1, source_target_pairs={{0,1},{1,0},{2,3},{3,2},{4,5},{5,4},{6,7},{7,6}} | collective-permute-start | bytes 11010056 | tf_op jit(solution)/shard_map/ppermute | solution.py:360
  292.7 41.3 %collective-permute-start.13 = (bf16[512,896]{1,0:T(8,128)(2,1)}, bf16[512,896]{1,0:T(8,128)(2,1)S(1)}, u32[]{:S(2)}, u32[]{:S(2)}) collective-permute-start(bf16[512,896]{1,0:T(8,128)(2,1)} %norm_grad.3), channel_id=1, source_target_pairs={{0,4},{4,0},{1,5},{5,1},{2,6},{6,2},{3,7},{7,3}} | collective-permute-start | bytes 2752520 | tf_op jit(solution)/shard_map/ppermute | solution.py:395
  332.6 21.9 %collective-permute-start.8 = (bf16[512,896]{1,0:T(8,128)(2,1)}, bf16[512,896]{1,0:T(8,128)(2,1)S(1)}, u32[]{:S(2)}, u32[]{:S(2)}) collective-permute-start(bf16[512,896]{1,0:T(8,128)(2,1)} %norm_grad.2), channel_id=1, source_target_pairs={{0,4},{4,0},{1,5},{5,1},{2,6},{6,2},{3,7},{7,3}} | collective-permute-start | bytes 2752520 | tf_op jit(solution)/shard_map/ppermute | solution.py:407
  335.4 43.2 %collective-permute-start.15 = (bf16[1024,896]{1,0:T(8,128)(2,1)}, bf16[1024,896]{1,0:T(8,128)(2,1)}, u32[]{:S(2)}, u32[]{:S(2)}) collective-permute-start(bf16[1024,896]{1,0:T(8,128)(2,1)} %pad_maximum_fusion.1.refs_0_), channel_id=1, source_target_pairs={{0,2},{2,0},{1,3},{3,1},{4,6},{6,4},{5,7},{7,5}} | collective-permute-start | bytes 5505032 | tf_op jit(solution)/shard_map/ppermute | solution.py:414
  355.8 60.3 %collective-permute-start.9 = (bf16[1024,896]{1,0:T(8,128)(2,1)S(1)}, bf16[1024,896]{1,0:T(8,128)(2,1)}, u32[]{:S(2)}, u32[]{:S(2)}) collective-permute-start(bf16[1024,896]{1,0:T(8,128)(2,1)S(1)} %pad_maximum_fusion.refs_4_), channel_id=1, source_target_pairs={{0,2},{2,0},{1,3},{3,1},{4,6},{6,4},{5,7},{7,5}} | collective-permute-start | bytes 5505032 | tf_op jit(solution)/shard_map/ppermute | solution.py:414
  361.7 54.4 %copy-start.15 = (bf16[2048,896]{1,0:T(8,128)(2,1)S(1)}, bf16[2048,896]{1,0:T(8,128)(2,1)}, u32[]{:S(2)}) copy-start(bf16[2048,896]{1,0:T(8,128)(2,1)} %all-gather.8.cloned.1.call-done) | copy-start | bytes 11010052
  361.7 225.8 %collective-permute-start.22 = (f32[608,896]{1,0:T(8,128)}, f32[608,896]{1,0:T(8,128)S(1)}, u32[]{:S(2)}, u32[]{:S(2)}) collective-permute-start(f32[608,896]{1,0:T(8,128)} %get-tuple-element.45), channel_id=1, source_target_pairs={{0,4},{4,0},{1,5},{5,1},{2,6},{6,2},{3,7},{7,3}} | collective-permute-start | bytes 6537224 | tf_op jit(solution)/shard_map/ppermute | solution.py:388
  365.6 57.7 %slice-start.4 = ((s8[4980736]{0:T(1024)(128)(4,1)}), s8[4194304]{0:T(1024)(128)(4,1)S(1)}, s32[]{:S(2)}) async-start(s8[4980736]{0:T(1024)(128)(4,1)} %bitcast.116), calls=%async_computation.7 | async-start | bytes 8388608
  369.3 54.1 %slice-start.5 = ((s8[4980736]{0:T(1024)(128)(4,1)}), s8[786432]{0:T(1024)(128)(4,1)S(1)}, s32[]{:S(2)}) async-start(s8[4980736]{0:T(1024)(128)(4,1)} %bitcast.116), calls=%async_computation.8 | async-start | bytes 1572864
  369.3 61.2 %collective-permute-start.14 = (bf16[1024,896]{1,0:T(8,128)(2,1)}, bf16[1024,896]{1,0:T(8,128)(2,1)S(1)}, u32[]{:S(2)}, u32[]{:S(2)}) collective-permute-start(bf16[1024,896]{1,0:T(8,128)(2,1)} %pad_maximum_fusion.1.refs_0_), channel_id=1, source_target_pairs={{0,1},{1,0},{2,3},{3,2},{4,5},{5,4},{6,7},{7,6}} | collective-permute-start | bytes 5505032 | tf_op jit(solution)/shard_map/ppermute | solution.py:413
  369.3 61.7 %collective-permute-start.17 = (bf16[1024,896]{1,0:T(8,128)(2,1)S(1)}, bf16[1024,896]{1,0:T(8,128)(2,1)S(1)}, u32[]{:S(2)}, u32[]{:S(2)}) collective-permute-start(bf16[1024,896]{1,0:T(8,128)(2,1)S(1)} %pad_maximum_fusion.refs_4_), channel_id=1, source_target_pairs={{0,1},{1,0},{2,3},{3,2},{4,5},{5,4},{6,7},{7,6}} | collective-permute-start | bytes 5505032 | tf_op jit(solution)/shard_map/ppermute | solution.py:413
  378.6 53.8 %collective-permute-start.16 = (bf16[1024,896]{1,0:T(8,128)(2,1)}, bf16[1024,896]{1,0:T(8,128)(2,1)S(1)}, u32[]{:S(2)}, u32[]{:S(2)}) collective-permute-start(bf16[1024,896]{1,0:T(8,128)(2,1)} %collective-permute-done.15.refs_2_), channel_id=1, source_target_pairs={{0,1},{1,0},{2,3},{3,2},{4,5},{5,4},{6,7},{7,6}} | collective-permute-start | bytes 5505032 | tf_op jit(solution)/shard_map/ppermute | solution.py:415
  416.1 16.9 %collective-permute-start.18 = (bf16[1024,896]{1,0:T(8,128)(2,1)}, bf16[1024,896]{1,0:T(8,128)(2,1)S(1)}, u32[]{:S(2)}, u32[]{:S(2)}) collective-permute-start(bf16[1024,896]{1,0:T(8,128)(2,1)} %collective-permute-done.9.refs_6_), channel_id=1, source_target_pairs={{0,1},{1,0},{2,3},{3,2},{4,5},{5,4},{6,7},{7,6}} | collective-permute-start | bytes 5505032 | tf_op jit(solution)/shard_map/ppermute | solution.py:415
  430.4 74.6 %collective-permute-start.23 = (f32[608,896]{1,0:T(8,128)}, f32[608,896]{1,0:T(8,128)}, u32[]{:S(2)}, u32[]{:S(2)}) collective-permute-start(f32[608,896]{1,0:T(8,128)} %get-tuple-element.43), channel_id=1, source_target_pairs={{0,4},{4,0},{1,5},{5,1},{2,6},{6,2},{3,7},{7,3}} | collective-permute-start | bytes 6537224 | tf_op jit(solution)/shard_map/ppermute | solution.py:396
  431.0 142.9 %collective-permute-start.21 = (f32[896,1216]{0,1:T(8,128)}, f32[896,1216]{0,1:T(8,128)}, u32[]{:S(2)}, u32[]{:S(2)}) collective-permute-start(f32[896,1216]{0,1:T(8,128)} %convolution_add_fusion), channel_id=1, source_target_pairs={{0,4},{4,0},{1,5},{5,1},{2,6},{6,2},{3,7},{7,3}} | collective-permute-start | bytes 13074440 | tf_op jit(solution)/shard_map/ppermute | solution.py:408
  432.5 147.5 %collective-permute-start.10 = (f32[512,896]{1,0:T(8,128)S(1)}, f32[512,896]{1,0:T(8,128)}, u32[]{:S(2)}, u32[]{:S(2)}) collective-permute-start(f32[512,896]{1,0:T(8,128)S(1)} %bitcast_add_fusion.4), channel_id=1, source_target_pairs={{0,2},{2,0},{1,3},{3,1},{4,6},{6,4},{5,7},{7,5}} | collective-permute-start | bytes 5505032 | tf_op jit(solution)/shard_map/ppermute | solution.py:366
  433.1 147.0 %collective-permute-start.20 = (f32[512,896]{1,0:T(8,128)}, f32[512,896]{1,0:T(8,128)}, u32[]{:S(2)}, u32[]{:S(2)}) collective-permute-start(f32[512,896]{1,0:T(8,128)} %bitcast_add_fusion), channel_id=1, source_target_pairs={{0,2},{2,0},{1,3},{3,1},{4,6},{6,4},{5,7},{7,5}} | collective-permute-start | bytes 5505032 | tf_op jit(solution)/shard_map/ppermute | solution.py:366
  505.0 75.0 %copy-start.7 = (bf16[512,896]{1,0:T(8,128)(2,1)S(1)}, bf16[512,896]{1,0:T(8,128)(2,1)}, u32[]{:S(2)}) copy-start(bf16[512,896]{1,0:T(8,128)(2,1)} %get-tuple-element.25.x_ref) | copy-start | bytes 2752516
  (33 other events, 325.0 us)
Sparse Core Ops, SparseCore 0:
  9.5 71.9 all-gather.3
  83.6 34.4 all-gather.5
  134.4 28.6 all-gather.7

commit v2 on v1

--- a/solution.py
+++ b/solution.py
@@ -138,7 +138,38 @@
     )(kept, got, away, gain)
 
 
-def dx_kernel(place_ref, part_ref, got_ref, away_ref, x_ref, grad_ref, gain_ref, dx_ref):
+def take_piece(piece_refs, held, sems):
+    step = pl.program_id(0)
+
+    @pl.when(step == 0)
+    def _():
+        for i, piece_ref in enumerate(piece_refs):
+            pltpu.make_async_copy(piece_ref, held.at[i], sems.at[i]).start()
+
+    pltpu.make_async_copy(piece_refs[0], held.at[step], sems.at[step]).wait()
+    return held[step]
+
+
+def join_kernel(*refs):
+    *piece_refs, out_ref, held, sems = refs
+    out_ref[...] = take_piece(piece_refs, held, sems)
+
+
+def join(pieces):
+    (rows, dim), count, kind = pieces[0].shape, len(pieces), pieces[0].dtype
+    return pl.pallas_call(
+        join_kernel,
+        out_shape=jax.ShapeDtypeStruct((count * rows, dim), kind),
+        grid=(count,),
+        in_specs=[pl.BlockSpec(memory_space=pl.ANY)] * count,
+        out_specs=pl.BlockSpec((rows, dim), lambda i: (i, 0)),
+        scratch_shapes=[pltpu.VMEM((count, rows, dim), kind), pltpu.SemaphoreType.DMA((count,))],
+        cost_estimate=pl.CostEstimate(flops=2_000_000_000, bytes_accessed=count * rows * dim * 4, transcendentals=0),
+        name="join",
+    )(*pieces)
+
+
+def dx_kernel(part_ref, got_ref, away_ref, x_ref, grad_ref, gain_ref, dx_ref):
     d_normed = (part_ref[...] + got_ref[...]) + away_ref[...]
     x = x_ref[...].astype(jnp.float32)
     inv_rms = lax.rsqrt(jnp.mean(x * x, axis=-1, keepdims=True) + NORM_EPS)
@@ -148,29 +179,26 @@
     dx_ref[...] = (grad_ref[...].astype(jnp.float32) + d_norm_in).astype(dx_ref.dtype)
 
 
-def norm_grad(place, part, got, away, x, grad, chunk, gain):
+def norm_grad(part, got, away, x, grad, chunk, gain):
     rows, dim = away.shape
     tile = rows // 2
-    plain = pl.BlockSpec((tile, dim), lambda i, p: (i, 0))
+    plain = pl.BlockSpec((tile, dim), lambda i: (i, 0))
     return pl.pallas_call(
         dx_kernel,
         out_shape=jax.ShapeDtypeStruct((rows, dim), x.dtype),
-        grid_spec=pltpu.PrefetchScalarGridSpec(
-            num_scalar_prefetch=1,
-            grid=(2,),
-            in_specs=[
-                pl.BlockSpec((None, None, tile, dim), lambda i, p: (p[0], p[1], i, 0)),
-                pl.BlockSpec((None, tile, dim), lambda i, p: (p[0], i, 0)),
-                plain,
-                plain,
-                pl.BlockSpec((tile, dim), lambda i, p: (2 * chunk + i, 0)),
-                pl.BlockSpec((1, dim), lambda i, p: (0, 0)),
-            ],
-            out_specs=plain,
-        ),
+        grid=(2,),
+        in_specs=[
+            pl.BlockSpec((None, None, tile, dim), lambda i: (0, 0, i, 0)),
+            pl.BlockSpec((None, tile, dim), lambda i: (0, i, 0)),
+            plain,
+            plain,
+            pl.BlockSpec((tile, dim), lambda i: (2 * chunk + i, 0)),
+            pl.BlockSpec((1, dim), lambda i: (0, 0)),
+        ],
+        out_specs=plain,
         cost_estimate=pl.CostEstimate(flops=3_000_000_000, bytes_accessed=rows * dim * 18, transcendentals=rows),
         name="norm_grad",
-    )(place, part, got, away, x, grad, gain)
+    )(part, got, away, x, grad, gain)
 
 
 def table_kernel(start_ref, key_ref, flip_ref, *refs):
@@ -321,14 +349,16 @@
         rank, replica = lax.axis_index("tensor"), lax.axis_index("data")
         chip, core = rank // 2, rank % 2
         gain_f32 = norm_gain.astype(jnp.float32)[None]
-        place = jnp.stack([chip, core]).astype(jnp.int32)
         places = token_ids.reshape(2, 2, 2, part)
         places = jnp.where(chip == 0, places[::-1], places)
         places = jnp.where(core == 0, places[:, ::-1], places)
         look = lookup_plan(places.transpose(2, 1, 0, 3).reshape(-1), rank, shard_rows)
 
         def gather(value):
-            return lax.all_gather(value, "tensor", axis=0, tiled=True)
+            from_chip = lax.ppermute(value, "tensor", CHIP_SWAP)
+            from_core = lax.ppermute(value, "tensor", CORE_SWAP)
+            from_both = lax.ppermute(from_chip, "tensor", CORE_SWAP)
+            return value, from_core, from_chip, from_both
 
         ids_other = lax.ppermute(token_ids, "data", DATA_SWAP)
         ids_low, ids_high = jnp.where(replica == 0, token_ids, ids_other), jnp.where(replica == 0, ids_other, token_ids)
@@ -336,8 +366,10 @@
         start, key = table_plan(ids_all, rank, shard_rows)
         flip = ((rank * 2 + replica) * part).astype(jnp.int32)[None]
 
-        grad_gathered = lax.all_gather(d_out.reshape(2, part, dim), "tensor", axis=1, tiled=True)
-        grad_all = [grad_gathered[0], grad_gathered[1]]
+        grad_all = []
+        for c in range(2):
+            pieces = gather(d_out[c * part : (c + 1) * part])
+            grad_all.append(join(pieces))
 
         looked, aways = [], []
         for c in range(2):
@@ -351,22 +383,20 @@
         for c in range(2):
             x, normed = norm(*looked[c], aways[c], gain_f32)
             embedded.append(x)
-            normed_all.append(gather(after(normed, grad_gathered)))
-        normed_all[0] = after(normed_all[0], key)
+            pieces = gather(normed)
+            normed_all.append(join(pieces))
 
         def core_sum(value):
             value = value.reshape(2, 2, part, dim)
-            send = lax.dynamic_index_in_dim(value, 1 - core, 1, keepdims=False)
-            return value, lax.ppermute(send, "tensor", CORE_SWAP)
+            return value, lax.ppermute(value[:, 1], "tensor", CORE_SWAP)
 
         def chip_sum(value, got, wait_for=None):
-            mine = lax.dynamic_slice(value, (1 - chip, core, 0, 0), (1, 1, part, dim)).reshape(part, dim)
-            away = mine + lax.dynamic_index_in_dim(got, 1 - chip, 0, keepdims=False)
+            away = value[1, 0] + got[1]
             away = away if wait_for is None else after(away, wait_for)
             return value, got, lax.ppermute(away, "tensor", CHIP_SWAP)
 
         def up(c):
-            return dot(normed_all[c], w_in, ROWS_BY_COLS).astype(jnp.bfloat16)
+            return normed_all[c], dot(normed_all[c], w_in, ROWS_BY_COLS).astype(jnp.bfloat16)
 
         def down(c, pre_gelu):
             gelu_pull = jax.vjp(gelu_tanh, pre_gelu.astype(jnp.float32))[1]
@@ -378,10 +408,9 @@
         def act(pre_gelu):
             return gelu_tanh(pre_gelu.astype(jnp.float32)).astype(jnp.bfloat16)
 
-        pre_0 = up(0)
-        grad_pre_0, norm_part_0, d_normed_0 = down(0, pre_0)
-        normed_all[1] = after(normed_all[1], norm_part_0)
-        pre_1 = up(1)
+        normed_0, pre_0 = up(0)
+        grad_pre_0, _, d_normed_0 = down(0, pre_0)
+        normed_1, pre_1 = up(1)
         hidden = [act(pre_0), act(pre_1)]
         grad_w_out = dot(hidden[0], grad_all[0], COLS_BY_COLS) + dot(hidden[1], grad_all[1], COLS_BY_COLS)
         cut = grad_w_out.shape[0] // 2
@@ -389,14 +418,14 @@
         grad_pre_1, _, d_normed_1 = down(1, after(pre_1, grad_w_out))
 
         def to_dx(c, sums):
-            return norm_grad(place, *sums, embedded[c], d_out, c, gain_f32)
+            return norm_grad(*sums, embedded[c], d_out, c, gain_f32)
 
         dx_0 = to_dx(0, chip_sum(*d_normed_0))
         crossed_0 = lax.ppermute(dx_0, "data", DATA_SWAP)
         other_out_1 = lax.ppermute(after(grad_w_out[cut:], dx_0), "data", DATA_SWAP)
 
         grad_pre = [after(g, dx_0) for g in (grad_pre_0, grad_pre_1)]
-        grad_w_in = dot(normed_all[0], grad_pre[0], COLS_BY_COLS) + dot(normed_all[1], grad_pre[1], COLS_BY_COLS)
+        grad_w_in = dot(normed_0, grad_pre[0], COLS_BY_COLS) + dot(normed_1, grad_pre[1], COLS_BY_COLS)
 
         y_sums = []
         for c in range(2):
@@ -421,8 +450,7 @@
 
         block_out = []
         for c, (value, got, away) in enumerate(y_sums):
-            mine = lax.dynamic_slice(value, (chip, core, 0, 0), (1, 1, part, dim)).reshape(part, dim)
-            mlp_out = (mine + lax.dynamic_index_in_dim(got, chip, 0, keepdims=False)) + after(away, grad_table)
+            mlp_out = (value[0, 0] + got[0]) + after(away, grad_table)
             block_out.append((embedded[c].astype(jnp.float32) + mlp_out).astype(jnp.bfloat16))
         block_out = jnp.concatenate(block_out)
         grad_w_in = grad_w_in + after(other_in, grad_table)

time: 607 us -> 593 us (0.977)
  waiting for transfers between devices: 264 us -> 246 us
  Pallas kernels: 124 us -> 137 us
  between operations: 14.6 us -> 1.93 us
  matrix products: 103 us -> 91.6 us
  starting transfers between devices: 18.1 us -> 26.7 us
  other arithmetic: 47.7 us -> 55.1 us
    ppermute x2, waiting for transfers between devices: 68.2 us -> 27.3 us  [per_device(): aways.append(lax.ppermute(kept[:part] + got[:part], 'tensor', CHIP_SWAP))]
    ppermute x4 -> x16, waiting for transfers between devices: 0.01 us -> 39.9 us  [the longest x4 39.9 us: gather(): from_chip = lax.ppermute(value, 'tensor', CHIP_SWAP)]
    pallas_call x0 -> x4, Pallas kernels: none -> 14.3 us  [join(): pl.pallas_call(join_kernel, out_shape=jax.ShapeDtypeStruct((count * rows,...]
    dot_general x12, matrix products: 103 us -> 91.6 us  [dot(): return lax.dot_general(a, b, dims, preferred_element_type=jnp.float32)]
    ppermute x2, waiting for transfers between devices: 46.3 us -> 36.5 us  [per_device(): from_chip = lax.ppermute(pair, 'tensor', CHIP_SWAP)]
    convert_element_type x0 -> x1, other arithmetic: none -> 7.2 us  [down(): grad_pre = gelu_pull(grad_hidden)[0].astype(jnp.bfloat16)]
    ppermute x4 -> x16, starting transfers between devices: 0.52 us -> 6.61 us  [the longest x4 5.02 us: gather(): from_chip = lax.ppermute(value, 'tensor', CHIP_SWAP)]
    unnamed x78 -> x86, local copies, waits for them, and re-layouts: 13.1 us -> 10.2 us
  transfers between devices with their start and end apart: 27 -> 36, of which waited for: 10 -> 11; matrix products, arithmetic and copies ran while one was open for 27% -> 27% of each run, Pallas kernels for 21% -> 22%
where the time goes in v2:
time: 593 us; the launch traced here: 584 us
  waiting for transfers between devices  246 us (41%)
  Pallas kernels  137 us (23%)
  matrix products  91.6 us (15%)
  other arithmetic  55.1 us (9%)
  starting transfers between devices  26.7 us (5%)
  local copies, waits for them, and re-layouts  26.2 us (4%)
    dot_general x12, matrix products, dot(): return lax.dot_general(a, b, dims, preferred_element_type=jnp.float32)  91.6 us
    pallas_call x1, Pallas kernels, table_grad(): pl.pallas_call(table_kernel, out_shape=jax.ShapeDtypeStruct((shard_rows,...  70.5 us
    ppermute x1, waiting for transfers between devices, per_device(): other_in = lax.ppermute(after(grad_w_in, dx_1), 'data', DATA_SWAP)  66.2 us
    ppermute x4, waiting for transfers between devices, chip_sum(): return (value, got, lax.ppermute(away, 'tensor', CHIP_SWAP))  59 us
    ppermute x4, waiting for transfers between devices, gather(): from_chip = lax.ppermute(value, 'tensor', CHIP_SWAP)  39.9 us
    pallas_call x4, Pallas kernels, lookup(): pl.pallas_call(functools.partial(lookup_kernel, base), out_shape=jax.Shap...  37.1 us
    ppermute x2, waiting for transfers between devices, per_device(): from_chip = lax.ppermute(pair, 'tensor', CHIP_SWAP)  36.5 us
    ppermute x2, waiting for transfers between devices, per_device(): aways.append(lax.ppermute(kept[:part] + got[:part], 'tensor', CHIP_SWAP))  27.3 us
  transfers between devices with their start and end apart: 36, of which 11 were waited for; matrix products, arithmetic and copies ran while one was open for 27% of the time, Pallas kernels for 22%

profile of v2, /device:TPU:0, one launch (start us, length us, event | category | flops | bytes accessed | tf_op | source)
XLA Modules:
  0.0 584.2 jit_solution(6993898125881190255)
XLA Ops:
  3.7 9.2 %lookup.5 = bf16[1024,896]{1,0:T(8,128)(2,1)} custom-call(s32[4096]{0:T(1024)} %bitcast.127, s32[16]{0:T(128)} %reduce_sum.18.count_ref, s32[128,32]{1,0:T(8,128)} %broadcast_add_fusion.code_ref, bf16[37984,896]{1,0:T(8,128)(2,1)} %table_ref.7), custom_call_target="tpu_custom_call" | custom-call | flops 5120000000 | bytes 16515072 | tf_op jit(solution)/shard_map/lookup/pallas_call | solution.py:97
  13.8 9.3 %lookup.7 = bf16[1024,896]{1,0:T(8,128)(2,1)} custom-call(s32[4096]{0:T(1024)} %bitcast.128, s32[16]{0:T(128)} %reduce_sum.18.count_ref, s32[128,32]{1,0:T(8,128)} %broadcast_add_fusion.code_ref, bf16[37984,896]{1,0:T(8,128)(2,1)} %table_ref.7), custom_call_target="tpu_custom_call" | custom-call | flops 5120000000 | bytes 16515072 | tf_op jit(solution)/shard_map/lookup/pallas_call | solution.py:97
  28.7 9.3 %lookup.4.kept_ref = bf16[1024,896]{1,0:T(8,128)(2,1)} custom-call(s32[4096]{0:T(1024)} %bitcast.129, s32[16]{0:T(128)} %reduce_sum.18.count_ref, s32[128,32]{1,0:T(8,128)} %broadcast_add_fusion.code_ref, bf16[37984,896]{1,0:T(8,128)(2,1)} %table_ref.7), custom_call_target="tpu_custom_call" | custom-call | flops 5120000000 | bytes 16515072 | tf_op jit(solution)/shard_map/lookup/pallas_call | solution.py:97
  42.5 7.7 %collective-permute-done.15.refs_2_ = bf16[512,896]{1,0:T(8,128)(2,1)} collective-permute-done((bf16[512,896]{1,0:T(8,128)(2,1)}, bf16[512,896]{1,0:T(8,128)(2,1)}, u32[]{:S(2)}, u32[]{:S(2)}) %collective-permute-start.15) | collective-permute-done | bytes 917536 | tf_op jit(solution)/shard_map/ppermute | solution.py:358
  50.2 9.3 %lookup.6.kept_ref = bf16[1024,896]{1,0:T(8,128)(2,1)} custom-call(s32[4096]{0:T(1024)} %bitcast.130, s32[16]{0:T(128)} %reduce_sum.18.count_ref, s32[128,32]{1,0:T(8,128)} %broadcast_add_fusion.code_ref, bf16[37984,896]{1,0:T(8,128)(2,1)} %table_ref.7), custom_call_target="tpu_custom_call" | custom-call | flops 5120000000 | bytes 16515072 | tf_op jit(solution)/shard_map/lookup/pallas_call | solution.py:97
  60.1 9.8 %collective-permute-done.7.refs_2_ = bf16[512,896]{1,0:T(8,128)(2,1)} collective-permute-done((bf16[512,896]{1,0:T(8,128)(2,1)S(1)}, bf16[512,896]{1,0:T(8,128)(2,1)}, u32[]{:S(2)}, u32[]{:S(2)}) %collective-permute-start.7) | collective-permute-done | bytes 917536 | tf_op jit(solution)/shard_map/ppermute | solution.py:358
  72.8 16.0 %collective-permute-done.1.away_ref = bf16[512,896]{1,0:T(8,128)(2,1)} collective-permute-done((bf16[512,896]{1,0:T(8,128)(2,1)}, bf16[512,896]{1,0:T(8,128)(2,1)}, u32[]{:S(2)}, u32[]{:S(2)}) %collective-permute-start.1) | collective-permute-done | bytes 917536 | tf_op jit(solution)/shard_map/ppermute | solution.py:380
  101.1 11.3 %collective-permute-done.10.away_ref = bf16[512,896]{1,0:T(8,128)(2,1)} collective-permute-done((bf16[512,896]{1,0:T(8,128)(2,1)}, bf16[512,896]{1,0:T(8,128)(2,1)}, u32[]{:S(2)}, u32[]{:S(2)}) %collective-permute-start.10) | collective-permute-done | bytes 917536 | tf_op jit(solution)/shard_map/ppermute | solution.py:380
  117.0 15.0 %collective-permute-done.3.refs_2_ = bf16[512,896]{1,0:T(8,128)(2,1)} collective-permute-done((bf16[512,896]{1,0:T(8,128)(2,1)}, bf16[512,896]{1,0:T(8,128)(2,1)}, u32[]{:S(2)}, u32[]{:S(2)}) %collective-permute-start.3) | collective-permute-done | bytes 917536 | tf_op jit(solution)/shard_map/ppermute | solution.py:358
  132.0 10.2 %fusion.48 = f32[2048,1216]{0,1:T(8,128)} fusion(bf16[2048,896]{1,0:T(8,128)(2,1)} %join.5, bf16[1216,896]{1,0:T(8,128)(2,1)} %param.10), kind=kOutput, calls=%fused_computation.97 | convolution fusion | flops 4462739456 | bytes 15810560 | tf_op jit(solution)/shard_map/dot_general | solution.py:335
  142.7 7.4 %collective-permute-done.12.refs_2_ = bf16[512,896]{1,0:T(8,128)(2,1)} collective-permute-done((bf16[512,896]{1,0:T(8,128)(2,1)}, bf16[512,896]{1,0:T(8,128)(2,1)}, u32[]{:S(2)}, u32[]{:S(2)}) %collective-permute-start.12) | collective-permute-done | bytes 917536 | tf_op jit(solution)/shard_map/ppermute | solution.py:358
  153.8 7.8 %convolution_convert_fusion.1 = bf16[2048,1216]{0,1:T(8,128)(2,1)S(1)} fusion(bf16[2048,896]{1,0:T(8,128)(2,1)} %join.4, bf16[896,1216]{0,1:T(8,128)(2,1)S(1)} %copy-done), kind=kOutput, calls=%fused_computation.39 | convolution fusion | flops 4465229824 | bytes 10829824 | tf_op jit(solution)/shard_map/dot_general | solution.py:335
  161.7 11.9 %fusion.4 = bf16[2048,1216]{0,1:T(8,128)(2,1)S(1)} fusion(bf16[2048,1216]{0,1:T(8,128)(2,1)S(1)} %convolution_convert_fusion.1, bf16[2048,896]{1,0:T(8,128)(2,1)S(1)} %copy-done.26, bf16[1216,896]{1,0:T(8,128)(2,1)S(1)} %copy-done.17), kind=kOutput, calls=%fused_computation.17 | convolution fusion | flops 4515037184 | bytes 15810560 | tf_op jit(solution)/shard_map/dot_general | solution.py:335
  173.6 5.8 fusion.50
  188.4 8.2 %convolution_convert_fusion = bf16[2048,1216]{0,1:T(8,128)(2,1)S(1)} fusion(bf16[2048,896]{1,0:T(8,128)(2,1)} %join.6, bf16[896,1216]{0,1:T(8,128)(2,1)S(1)} %copy-done), kind=kOutput, calls=%fused_computation.38 | convolution fusion | flops 4465229824 | bytes 10829824 | tf_op jit(solution)/shard_map/dot_general | solution.py:335
  196.7 6.3 %fusion.44 = f32[1216,896]{1,0:T(8,128)S(1)} fusion(bf16[2048,896]{1,0:T(8,128)(2,1)S(1)} %copy-done.28, bf16[2048,1216]{0,1:T(8,128)(2,1)S(1)} %convolution_convert_fusion), kind=kOutput, calls=%fused_computation.94 | convolution fusion | flops 4487643136 | bytes 13008896 | tf_op jit(solution)/shard_map/dot_general | solution.py:335
  203.0 7.9 %convolution_add_fusion.1 = f32[1216,896]{1,0:T(8,128)} fusion(f32[1216,896]{1,0:T(8,128)S(1)} %fusion.44, bf16[2048,896]{1,0:T(8,128)(2,1)S(1)} %copy-done.27, bf16[2048,1216]{0,1:T(8,128)(2,1)S(1)} %bitcast.137), kind=kOutput, calls=%fused_computation.42 | convolution fusion | flops 4488732672 | bytes 17367040 | tf_op jit(solution)/shard_map/dot_general | solution.py:335
  211.0 7.2 %fusion.7 = bf16[2048,1216]{0,1:T(8,128)(2,1)S(1)} fusion(bf16[2048,1216]{0,1:T(8,128)(2,1)S(1)} %convolution_convert_fusion, f32[2048,1216]{0,1:T(8,128)S(1)} %bitcast.118), kind=kLoop, calls=%fused_computation.20 | loop fusion | flops 52297728 | bytes 19922944 | tf_op jit(solution)/shard_map/convert_element_type | solution.py:404
  218.2 5.8 fusion.49
  227.3 7.8 %fusion.40 = f32[2048,896]{1,0:T(8,128)S(1)} fusion(bf16[1216,896]{1,0:T(8,128)(2,1)S(1)} %copy-done.18, bf16[2048,1216]{0,1:T(8,128)(2,1)S(1)} %bitcast.137), kind=kOutput, calls=%fused_computation.92 | convolution fusion | flops 4487643136 | bytes 14499840 | tf_op jit(solution)/shard_map/dot_general | solution.py:335
  235.1 4.9 fusion.30
  243.6 7.6 %fusion.42 = f32[2048,896]{1,0:T(8,128)S(1)} fusion(bf16[1216,896]{1,0:T(8,128)(2,1)S(1)} %copy-done.18, bf16[2048,1216]{0,1:T(8,128)(2,1)S(1)} %convolution_convert_fusion), kind=kOutput, calls=%fused_computation.93 | convolution fusion | flops 4487643136 | bytes 14499840 | tf_op jit(solution)/shard_map/dot_general | solution.py:335
  256.4 26.6 %collective-permute-done.24.away_ref = f32[512,896]{1,0:T(8,128)} collective-permute-done((f32[512,896]{1,0:T(8,128)S(1)}, f32[512,896]{1,0:T(8,128)}, u32[]{:S(2)}, u32[]{:S(2)}) %collective-permute-start.24) | collective-permute-done | bytes 1835040 | tf_op jit(solution)/shard_map/ppermute | solution.py:396
  288.9 32.4 %collective-permute-done.18.away_ref = f32[512,896]{1,0:T(8,128)S(1)} collective-permute-done((f32[512,896]{1,0:T(8,128)}, f32[512,896]{1,0:T(8,128)S(1)}, u32[]{:S(2)}, u32[]{:S(2)}) %collective-permute-start.18) | collective-permute-done | bytes 1835040 | tf_op jit(solution)/shard_map/ppermute | solution.py:396
  332.1 16.9 %collective-permute-done.19 = bf16[512,896]{1,0:T(8,128)(2,1)S(1)} collective-permute-done((bf16[512,896]{1,0:T(8,128)(2,1)}, bf16[512,896]{1,0:T(8,128)(2,1)S(1)}, u32[]{:S(2)}, u32[]{:S(2)}) %collective-permute-start.19) | collective-permute-done | bytes 917536 | tf_op jit(solution)/shard_map/ppermute | solution.py:436
  352.0 6.8 %sort.10 = (s32[8192]{0:T(1024)S(1)}, s32[8192]{0:T(1024)}) sort(s32[8192]{0:T(1024)S(1)} %iota_add_fusion, s32[8192]{0:T(1024)S(1)} %iota.20), dimensions={0}, to_apply=%region_1.2 | sort | flops 106496 | bytes 131072 | tf_op jit(solution)/shard_map/sort | solution.py:297
  374.3 36.5 %collective-permute-done.20.refs_6_ = bf16[1024,896]{1,0:T(8,128)(2,1)} collective-permute-done((bf16[1024,896]{1,0:T(8,128)(2,1)S(1)}, bf16[1024,896]{1,0:T(8,128)(2,1)}, u32[]{:S(2)}, u32[]{:S(2)}) %collective-permute-start.20) | collective-permute-done | bytes 1835040 | tf_op jit(solution)/shard_map/ppermute | solution.py:443
  410.8 5.3 fusion.51
  416.2 6.9 %convolution_add_fusion = f32[896,1216]{0,1:T(8,128)} fusion(f32[896,1216]{0,1:T(8,128)S(1)} %fusion.51, bf16[2048,1216]{0,1:T(8,128)(2,1)S(1)} %bitcast.135, bf16[2048,896]{1,0:T(8,128)(2,1)S(1)} %copy-done.24), kind=kOutput, calls=%fused_computation.41 | convolution fusion | flops 4463828992 | bytes 17367040 | tf_op jit(solution)/shard_map/dot_general | solution.py:335
  429.8 70.5 %table_grad.1 = f32[37984,896]{1,0:T(8,128)} custom-call(s32[20]{0:T(128)} %convert_reduce_fusion.start_ref, s32[8192]{0:T(1024)} %copy-done.15, s32[1]{0:T(128)} %bitcast.14.flip_ref, bf16[1024,896]{1,0:T(8,128)(2,1)} %pad_maximum_fusion.1.refs_0_, bf16[1024,896]{1,0:T(8,128)(2,1)} %copy-done.19, bf16[1024,896]{1,0:T(8,128)(2,1)} %collective-permute-done.27.refs_2_, ...), custom_call_target="tpu_custom_call" | custom-call | flops 60000002048 | bytes 136134656 | tf_op jit(solution)/shard_map/table_grad/pallas_call | solution.py:304
  500.3 66.2 %collective-permute-done.33 = f32[896,1216]{0,1:T(8,128)} collective-permute-done((f32[896,1216]{0,1:T(8,128)}, f32[896,1216]{0,1:T(8,128)}, u32[]{:S(2)}, u32[]{:S(2)}) %collective-permute-start.33) | collective-permute-done | bytes 4358176 | tf_op jit(solution)/shard_map/ppermute | solution.py:437
  566.6 6.1 %add.108 = f32[896,1216]{0,1:T(8,128)} add(f32[896,1216]{0,1:T(8,128)} %convolution_add_fusion, f32[896,1216]{0,1:T(8,128)} %collective-permute-done.33) | non-fusion elementwise | flops 1089536 | bytes 13074432 | tf_op jit(solution)/shard_map/add | solution.py:456
  (199 shorter events, 112.2 us)
Async XLA Ops:
  12.9 25.1 %collective-permute-start = (bf16[1024,896]{1,0:T(8,128)(2,1)}, bf16[1024,896]{1,0:T(8,128)(2,1)}, u32[]{:S(2)}, u32[]{:S(2)}) collective-permute-start(bf16[1024,896]{1,0:T(8,128)(2,1)} %lookup.5), channel_id=1, source_target_pairs={{0,1},{1,0},{2,3},{3,2},{4,5},{5,4},{6,7},{7,6}} | collective-permute-start | bytes 5505032 | tf_op jit(solution)/shard_map/ppermute | solution.py:377
  23.1 46.8 %collective-permute-start.9 = (bf16[1024,896]{1,0:T(8,128)(2,1)}, bf16[1024,896]{1,0:T(8,128)(2,1)}, u32[]{:S(2)}, u32[]{:S(2)}) collective-permute-start(bf16[1024,896]{1,0:T(8,128)(2,1)} %lookup.7), channel_id=1, source_target_pairs={{0,1},{1,0},{2,3},{3,2},{4,5},{5,4},{6,7},{7,6}} | collective-permute-start | bytes 5505032 | tf_op jit(solution)/shard_map/ppermute | solution.py:377
  25.7 24.5 %collective-permute-start.15 = (bf16[512,896]{1,0:T(8,128)(2,1)}, bf16[512,896]{1,0:T(8,128)(2,1)}, u32[]{:S(2)}, u32[]{:S(2)}) collective-permute-start(bf16[512,896]{1,0:T(8,128)(2,1)} %get-tuple-element.39.refs_0_), channel_id=1, source_target_pairs={{0,2},{2,0},{1,3},{3,1},{4,6},{6,4},{5,7},{7,5}} | collective-permute-start | bytes 2752520 | tf_op jit(solution)/shard_map/ppermute | solution.py:358
  28.7 41.2 %collective-permute-start.7 = (bf16[512,896]{1,0:T(8,128)(2,1)S(1)}, bf16[512,896]{1,0:T(8,128)(2,1)}, u32[]{:S(2)}, u32[]{:S(2)}) collective-permute-start(bf16[512,896]{1,0:T(8,128)(2,1)S(1)} %get-tuple-element.40.refs_0_), channel_id=1, source_target_pairs={{0,2},{2,0},{1,3},{3,1},{4,6},{6,4},{5,7},{7,5}} | collective-permute-start | bytes 2752520 | tf_op jit(solution)/shard_map/ppermute | solution.py:358
  40.5 48.3 %collective-permute-start.1 = (bf16[512,896]{1,0:T(8,128)(2,1)}, bf16[512,896]{1,0:T(8,128)(2,1)}, u32[]{:S(2)}, u32[]{:S(2)}) collective-permute-start(bf16[512,896]{1,0:T(8,128)(2,1)} %slice_add_fusion.1), channel_id=1, source_target_pairs={{0,2},{2,0},{1,3},{3,1},{4,6},{6,4},{5,7},{7,5}} | collective-permute-start | bytes 2752520 | tf_op jit(solution)/shard_map/ppermute | solution.py:380
  42.5 51.0 %collective-permute-start.14 = (bf16[512,896]{1,0:T(8,128)(2,1)}, bf16[512,896]{1,0:T(8,128)(2,1)}, u32[]{:S(2)}, u32[]{:S(2)}) collective-permute-start(bf16[512,896]{1,0:T(8,128)(2,1)} %get-tuple-element.39.refs_0_), channel_id=1, source_target_pairs={{0,1},{1,0},{2,3},{3,2},{4,5},{5,4},{6,7},{7,6}} | collective-permute-start | bytes 2752520 | tf_op jit(solution)/shard_map/ppermute | solution.py:359
  50.2 43.6 %collective-permute-start.16 = (bf16[512,896]{1,0:T(8,128)(2,1)}, bf16[512,896]{1,0:T(8,128)(2,1)}, u32[]{:S(2)}, u32[]{:S(2)}) collective-permute-start(bf16[512,896]{1,0:T(8,128)(2,1)} %collective-permute-done.15.refs_2_), channel_id=1, source_target_pairs={{0,1},{1,0},{2,3},{3,2},{4,5},{5,4},{6,7},{7,6}} | collective-permute-start | bytes 2752520 | tf_op jit(solution)/shard_map/ppermute | solution.py:360
  69.8 27.4 %collective-permute-start.6 = (bf16[512,896]{1,0:T(8,128)(2,1)S(1)}, bf16[512,896]{1,0:T(8,128)(2,1)}, u32[]{:S(2)}, u32[]{:S(2)}) collective-permute-start(bf16[512,896]{1,0:T(8,128)(2,1)S(1)} %get-tuple-element.40.refs_0_), channel_id=1, source_target_pairs={{0,1},{1,0},{2,3},{3,2},{4,5},{5,4},{6,7},{7,6}} | collective-permute-start | bytes 2752520 | tf_op jit(solution)/shard_map/ppermute | solution.py:359
  69.8 27.5 %collective-permute-start.8 = (bf16[512,896]{1,0:T(8,128)(2,1)}, bf16[512,896]{1,0:T(8,128)(2,1)}, u32[]{:S(2)}, u32[]{:S(2)}) collective-permute-start(bf16[512,896]{1,0:T(8,128)(2,1)} %collective-permute-done.7.refs_2_), channel_id=1, source_target_pairs={{0,1},{1,0},{2,3},{3,2},{4,5},{5,4},{6,7},{7,6}} | collective-permute-start | bytes 2752520 | tf_op jit(solution)/shard_map/ppermute | solution.py:360
  88.8 23.5 %collective-permute-start.10 = (bf16[512,896]{1,0:T(8,128)(2,1)}, bf16[512,896]{1,0:T(8,128)(2,1)}, u32[]{:S(2)}, u32[]{:S(2)}) collective-permute-start(bf16[512,896]{1,0:T(8,128)(2,1)} %slice_add_fusion), channel_id=1, source_target_pairs={{0,2},{2,0},{1,3},{3,1},{4,6},{6,4},{5,7},{7,5}} | collective-permute-start | bytes 2752520 | tf_op jit(solution)/shard_map/ppermute | solution.py:380
  93.5 38.5 %collective-permute-start.3 = (bf16[512,896]{1,0:T(8,128)(2,1)}, bf16[512,896]{1,0:T(8,128)(2,1)}, u32[]{:S(2)}, u32[]{:S(2)}) collective-permute-start(bf16[512,896]{1,0:T(8,128)(2,1)} %get-tuple-element.22.refs_0_), channel_id=1, source_target_pairs={{0,2},{2,0},{1,3},{3,1},{4,6},{6,4},{5,7},{7,5}} | collective-permute-start | bytes 2752520 | tf_op jit(solution)/shard_map/ppermute | solution.py:358
  101.0 49.1 %collective-permute-start.2 = (bf16[512,896]{1,0:T(8,128)(2,1)S(1)}, bf16[512,896]{1,0:T(8,128)(2,1)}, u32[]{:S(2)}, u32[]{:S(2)}) collective-permute-start(bf16[512,896]{1,0:T(8,128)(2,1)S(1)} %copy-done.23), channel_id=1, source_target_pairs={{0,1},{1,0},{2,3},{3,2},{4,5},{5,4},{6,7},{7,6}} | collective-permute-start | bytes 2752520 | tf_op jit(solution)/shard_map/ppermute | solution.py:359
  115.2 34.9 %collective-permute-start.12 = (bf16[512,896]{1,0:T(8,128)(2,1)}, bf16[512,896]{1,0:T(8,128)(2,1)}, u32[]{:S(2)}, u32[]{:S(2)}) collective-permute-start(bf16[512,896]{1,0:T(8,128)(2,1)} %get-tuple-element.23.refs_0_), channel_id=1, source_target_pairs={{0,2},{2,0},{1,3},{3,1},{4,6},{6,4},{5,7},{7,5}} | collective-permute-start | bytes 2752520 | tf_op jit(solution)/shard_map/ppermute | solution.py:358
  142.2 42.7 %collective-permute-start.11 = (bf16[512,896]{1,0:T(8,128)(2,1)}, bf16[512,896]{1,0:T(8,128)(2,1)}, u32[]{:S(2)}, u32[]{:S(2)}) collective-permute-start(bf16[512,896]{1,0:T(8,128)(2,1)} %get-tuple-element.23.refs_0_), channel_id=1, source_target_pairs={{0,1},{1,0},{2,3},{3,2},{4,5},{5,4},{6,7},{7,6}} | collective-permute-start | bytes 2752520 | tf_op jit(solution)/shard_map/ppermute | solution.py:359
  150.2 34.7 %collective-permute-start.13 = (bf16[512,896]{1,0:T(8,128)(2,1)}, bf16[512,896]{1,0:T(8,128)(2,1)}, u32[]{:S(2)}, u32[]{:S(2)}) collective-permute-start(bf16[512,896]{1,0:T(8,128)(2,1)} %collective-permute-done.12.refs_2_), channel_id=1, source_target_pairs={{0,1},{1,0},{2,3},{3,2},{4,5},{5,4},{6,7},{7,6}} | collective-permute-start | bytes 2752520 | tf_op jit(solution)/shard_map/ppermute | solution.py:360
  184.4 50.7 %collective-permute-start.23 = (f32[2,512,896]{2,1,0:T(8,128)}, f32[2,512,896]{2,1,0:T(8,128)}, u32[]{:S(2)}, u32[]{:S(2)}) collective-permute-start(f32[2,512,896]{2,1,0:T(8,128)} %slice_bitcast_fusion.1), channel_id=1, source_target_pairs={{0,1},{1,0},{2,3},{3,2},{4,5},{5,4},{6,7},{7,6}} | collective-permute-start | bytes 11010056 | tf_op jit(solution)/shard_map/ppermute | solution.py:391
  240.0 43.0 %collective-permute-start.24 = (f32[512,896]{1,0:T(8,128)S(1)}, f32[512,896]{1,0:T(8,128)}, u32[]{:S(2)}, u32[]{:S(2)}) collective-permute-start(f32[512,896]{1,0:T(8,128)S(1)} %fusion.30), channel_id=1, source_target_pairs={{0,2},{2,0},{1,3},{3,1},{4,6},{6,4},{5,7},{7,5}} | collective-permute-start | bytes 5505032 | tf_op jit(solution)/shard_map/ppermute | solution.py:396
  243.1 78.3 %collective-permute-start.18 = (f32[512,896]{1,0:T(8,128)}, f32[512,896]{1,0:T(8,128)S(1)}, u32[]{:S(2)}, u32[]{:S(2)}) collective-permute-start(f32[512,896]{1,0:T(8,128)} %fusion.31), channel_id=1, source_target_pairs={{0,2},{2,0},{1,3},{3,1},{4,6},{6,4},{5,7},{7,5}} | collective-permute-start | bytes 5505032 | tf_op jit(solution)/shard_map/ppermute | solution.py:396
  253.5 112.4 %collective-permute-start.5 = (f32[2,512,896]{2,1,0:T(8,128)}, f32[2,512,896]{2,1,0:T(8,128)}, u32[]{:S(2)}, u32[]{:S(2)}) collective-permute-start(f32[2,512,896]{2,1,0:T(8,128)} %slice_bitcast_fusion.3), channel_id=1, source_target_pairs={{0,1},{1,0},{2,3},{3,2},{4,5},{5,4},{6,7},{7,6}} | collective-permute-start | bytes 11010056 | tf_op jit(solution)/shard_map/ppermute | solution.py:391
  256.4 113.6 %collective-permute-start.31 = (f32[2,512,896]{2,1,0:T(8,128)}, f32[2,512,896]{2,1,0:T(8,128)}, u32[]{:S(2)}, u32[]{:S(2)}) collective-permute-start(f32[2,512,896]{2,1,0:T(8,128)} %slice_bitcast_fusion), channel_id=1, source_target_pairs={{0,1},{1,0},{2,3},{3,2},{4,5},{5,4},{6,7},{7,6}} | collective-permute-start | bytes 11010056 | tf_op jit(solution)/shard_map/ppermute | solution.py:391
  287.4 41.9 %collective-permute-start.25 = (bf16[512,896]{1,0:T(8,128)(2,1)}, bf16[512,896]{1,0:T(8,128)(2,1)S(1)}, u32[]{:S(2)}, u32[]{:S(2)}) collective-permute-start(bf16[512,896]{1,0:T(8,128)(2,1)} %norm_grad.3), channel_id=1, source_target_pairs={{0,4},{4,0},{1,5},{5,1},{2,6},{6,2},{3,7},{7,3}} | collective-permute-start | bytes 2752520 | tf_op jit(solution)/shard_map/ppermute | solution.py:424
  328.7 23.1 %collective-permute-start.22 = (s32[4096]{0:T(1024)S(1)}, s32[4096]{0:T(1024)S(1)}, u32[]{:S(2)}, u32[]{:S(2)}) collective-permute-start(s32[4096]{0:T(1024)S(1)} %copy-done.14), channel_id=1, source_target_pairs={{0,4},{4,0},{1,5},{5,1},{2,6},{6,2},{3,7},{7,3}} | collective-permute-start | bytes 49160 | tf_op jit(solution)/shard_map/ppermute | solution.py:363
  330.6 43.6 %collective-permute-start.27 = (bf16[1024,896]{1,0:T(8,128)(2,1)}, bf16[1024,896]{1,0:T(8,128)(2,1)}, u32[]{:S(2)}, u32[]{:S(2)}) collective-permute-start(bf16[1024,896]{1,0:T(8,128)(2,1)} %pad_maximum_fusion.1.refs_0_), channel_id=1, source_target_pairs={{0,2},{2,0},{1,3},{3,1},{4,6},{6,4},{5,7},{7,5}} | collective-permute-start | bytes 5505032 | tf_op jit(solution)/shard_map/ppermute | solution.py:443
  350.3 60.4 %collective-permute-start.20 = (bf16[1024,896]{1,0:T(8,128)(2,1)S(1)}, bf16[1024,896]{1,0:T(8,128)(2,1)}, u32[]{:S(2)}, u32[]{:S(2)}) collective-permute-start(bf16[1024,896]{1,0:T(8,128)(2,1)S(1)} %pad_maximum_fusion.refs_4_), channel_id=1, source_target_pairs={{0,2},{2,0},{1,3},{3,1},{4,6},{6,4},{5,7},{7,5}} | collective-permute-start | bytes 5505032 | tf_op jit(solution)/shard_map/ppermute | solution.py:443
  364.4 215.2 %collective-permute-start.34 = (f32[608,896]{1,0:T(8,128)}, f32[608,896]{1,0:T(8,128)S(1)}, u32[]{:S(2)}, u32[]{:S(2)}) collective-permute-start(f32[608,896]{1,0:T(8,128)} %get-tuple-element.37), channel_id=1, source_target_pairs={{0,4},{4,0},{1,5},{5,1},{2,6},{6,2},{3,7},{7,3}} | collective-permute-start | bytes 6537224 | tf_op jit(solution)/shard_map/ppermute | solution.py:417
  373.7 49.4 %collective-permute-start.26 = (bf16[1024,896]{1,0:T(8,128)(2,1)}, bf16[1024,896]{1,0:T(8,128)(2,1)S(1)}, u32[]{:S(2)}, u32[]{:S(2)}) collective-permute-start(bf16[1024,896]{1,0:T(8,128)(2,1)} %pad_maximum_fusion.1.refs_0_), channel_id=1, source_target_pairs={{0,1},{1,0},{2,3},{3,2},{4,5},{5,4},{6,7},{7,6}} | collective-permute-start | bytes 5505032 | tf_op jit(solution)/shard_map/ppermute | solution.py:442
  373.7 50.8 %collective-permute-start.29 = (bf16[1024,896]{1,0:T(8,128)(2,1)S(1)}, bf16[1024,896]{1,0:T(8,128)(2,1)S(1)}, u32[]{:S(2)}, u32[]{:S(2)}) collective-permute-start(bf16[1024,896]{1,0:T(8,128)(2,1)S(1)} %pad_maximum_fusion.refs_4_), channel_id=1, source_target_pairs={{0,1},{1,0},{2,3},{3,2},{4,5},{5,4},{6,7},{7,6}} | collective-permute-start | bytes 5505032 | tf_op jit(solution)/shard_map/ppermute | solution.py:442
  374.2 50.9 %collective-permute-start.28 = (bf16[1024,896]{1,0:T(8,128)(2,1)}, bf16[1024,896]{1,0:T(8,128)(2,1)S(1)}, u32[]{:S(2)}, u32[]{:S(2)}) collective-permute-start(bf16[1024,896]{1,0:T(8,128)(2,1)} %collective-permute-done.27.refs_2_), channel_id=1, source_target_pairs={{0,1},{1,0},{2,3},{3,2},{4,5},{5,4},{6,7},{7,6}} | collective-permute-start | bytes 5505032 | tf_op jit(solution)/shard_map/ppermute | solution.py:444
  423.1 77.3 %collective-permute-start.35 = (f32[608,896]{1,0:T(8,128)}, f32[608,896]{1,0:T(8,128)}, u32[]{:S(2)}, u32[]{:S(2)}) collective-permute-start(f32[608,896]{1,0:T(8,128)} %get-tuple-element.35), channel_id=1, source_target_pairs={{0,4},{4,0},{1,5},{5,1},{2,6},{6,2},{3,7},{7,3}} | collective-permute-start | bytes 6537224 | tf_op jit(solution)/shard_map/ppermute | solution.py:425
  424.6 142.0 %collective-permute-start.33 = (f32[896,1216]{0,1:T(8,128)}, f32[896,1216]{0,1:T(8,128)}, u32[]{:S(2)}, u32[]{:S(2)}) collective-permute-start(f32[896,1216]{0,1:T(8,128)} %convolution_add_fusion), channel_id=1, source_target_pairs={{0,4},{4,0},{1,5},{5,1},{2,6},{6,2},{3,7},{7,3}} | collective-permute-start | bytes 13074440 | tf_op jit(solution)/shard_map/ppermute | solution.py:437
  425.8 146.8 %collective-permute-start.21 = (f32[512,896]{1,0:T(8,128)}, f32[512,896]{1,0:T(8,128)S(1)}, u32[]{:S(2)}, u32[]{:S(2)}) collective-permute-start(f32[512,896]{1,0:T(8,128)} %fusion.32), channel_id=1, source_target_pairs={{0,2},{2,0},{1,3},{3,1},{4,6},{6,4},{5,7},{7,5}} | collective-permute-start | bytes 5505032 | tf_op jit(solution)/shard_map/ppermute | solution.py:396
  428.5 144.1 %collective-permute-start.32 = (f32[512,896]{1,0:T(8,128)}, f32[512,896]{1,0:T(8,128)}, u32[]{:S(2)}, u32[]{:S(2)}) collective-permute-start(f32[512,896]{1,0:T(8,128)} %fusion.25), channel_id=1, source_target_pairs={{0,2},{2,0},{1,3},{3,1},{4,6},{6,4},{5,7},{7,5}} | collective-permute-start | bytes 5505032 | tf_op jit(solution)/shard_map/ppermute | solution.py:396
  (46 other events, 876.6 us)

commit v3 on v2

--- a/solution.py
+++ b/solution.py
@@ -422,7 +422,8 @@
 
         dx_0 = to_dx(0, chip_sum(*d_normed_0))
         crossed_0 = lax.ppermute(dx_0, "data", DATA_SWAP)
-        other_out_1 = lax.ppermute(after(grad_w_out[cut:], dx_0), "data", DATA_SWAP)
+        other_out_1 = lax.ppermute(grad_w_out[cut : cut + 128], "data", DATA_SWAP)
+        other_out_2 = lax.ppermute(after(grad_w_out[cut + 128 :], dx_0), "data", DATA_SWAP)
 
         grad_pre = [after(g, dx_0) for g in (grad_pre_0, grad_pre_1)]
         grad_w_in = dot(normed_0, grad_pre[0], COLS_BY_COLS) + dot(normed_1, grad_pre[1], COLS_BY_COLS)
@@ -454,7 +455,7 @@
             block_out.append((embedded[c].astype(jnp.float32) + mlp_out).astype(jnp.bfloat16))
         block_out = jnp.concatenate(block_out)
         grad_w_in = grad_w_in + after(other_in, grad_table)
-        grad_w_out = grad_w_out + jnp.concatenate([other_out_0, after(other_out_1, grad_table)])
+        grad_w_out = grad_w_out + jnp.concatenate([other_out_0, other_out_1, after(other_out_2, grad_table)])
         return block_out, grad_table, grad_w_in, grad_w_out
 
     return jax.shard_map(

time: 593 us -> 584 us (0.985)
  waiting for transfers between devices: 246 us -> 232 us
    ppermute x1, waiting for transfers between devices: 66.2 us -> 56.3 us  [per_device(): other_in = lax.ppermute(after(grad_w_in, dx_1), 'data', DATA_SWAP)]
    ppermute x2, waiting for transfers between devices: 36.5 us -> 30.3 us  [per_device(): from_chip = lax.ppermute(pair, 'tensor', CHIP_SWAP)]
  transfers between devices with their start and end apart: 36 -> 37, of which waited for: 11 -> 12; matrix products, arithmetic and copies ran while one was open for 27% -> 28% of each run, Pallas kernels for 22% -> 22%
where the time goes in v3:
time: 584 us; the launch traced here: 575 us
  waiting for transfers between devices  232 us (40%)
  Pallas kernels  137 us (23%)
  matrix products  91.6 us (16%)
  other arithmetic  54.4 us (9%)
  starting transfers between devices  28.9 us (5%)
  local copies, waits for them, and re-layouts  28.8 us (5%)
    dot_general x12, matrix products, dot(): return lax.dot_general(a, b, dims, preferred_element_type=jnp.float32)  91.6 us
    pallas_call x1, Pallas kernels, table_grad(): pl.pallas_call(table_kernel, out_shape=jax.ShapeDtypeStruct((shard_rows,...  70.5 us
    ppermute x4, waiting for transfers between devices, chip_sum(): return (value, got, lax.ppermute(away, 'tensor', CHIP_SWAP))  59.1 us
    ppermute x1, waiting for transfers between devices, per_device(): other_in = lax.ppermute(after(grad_w_in, dx_1), 'data', DATA_SWAP)  56.3 us
    ppermute x4, waiting for transfers between devices, gather(): from_chip = lax.ppermute(value, 'tensor', CHIP_SWAP)  39.9 us
    pallas_call x4, Pallas kernels, lookup(): pl.pallas_call(functools.partial(lookup_kernel, base), out_shape=jax.Shap...  37.1 us
    ppermute x2, waiting for transfers between devices, per_device(): from_chip = lax.ppermute(pair, 'tensor', CHIP_SWAP)  30.3 us
    ppermute x2, waiting for transfers between devices, per_device(): aways.append(lax.ppermute(kept[:part] + got[:part], 'tensor', CHIP_SWAP))  27.3 us
  transfers between devices with their start and end apart: 37, of which 12 were waited for; matrix products, arithmetic and copies ran while one was open for 28% of the time, Pallas kernels for 22%

profile of v3, /device:TPU:0, one launch (start us, length us, event | category | flops | bytes accessed | tf_op | source)
XLA Modules:
  0.0 574.6 jit_solution(12448642350267958784)
XLA Ops:
  3.7 9.2 %lookup.5 = bf16[1024,896]{1,0:T(8,128)(2,1)} custom-call(s32[4096]{0:T(1024)} %bitcast.127, s32[16]{0:T(128)} %reduce_sum.18.count_ref, s32[128,32]{1,0:T(8,128)} %broadcast_add_fusion.code_ref, bf16[37984,896]{1,0:T(8,128)(2,1)} %table_ref.7), custom_call_target="tpu_custom_call" | custom-call | flops 5120000000 | bytes 16515072 | tf_op jit(solution)/shard_map/lookup/pallas_call | solution.py:97
  13.8 9.3 %lookup.7 = bf16[1024,896]{1,0:T(8,128)(2,1)} custom-call(s32[4096]{0:T(1024)} %bitcast.128, s32[16]{0:T(128)} %reduce_sum.18.count_ref, s32[128,32]{1,0:T(8,128)} %broadcast_add_fusion.code_ref, bf16[37984,896]{1,0:T(8,128)(2,1)} %table_ref.7), custom_call_target="tpu_custom_call" | custom-call | flops 5120000000 | bytes 16515072 | tf_op jit(solution)/shard_map/lookup/pallas_call | solution.py:97
  28.7 9.3 %lookup.4.kept_ref = bf16[1024,896]{1,0:T(8,128)(2,1)} custom-call(s32[4096]{0:T(1024)} %bitcast.129, s32[16]{0:T(128)} %reduce_sum.18.count_ref, s32[128,32]{1,0:T(8,128)} %broadcast_add_fusion.code_ref, bf16[37984,896]{1,0:T(8,128)(2,1)} %table_ref.7), custom_call_target="tpu_custom_call" | custom-call | flops 5120000000 | bytes 16515072 | tf_op jit(solution)/shard_map/lookup/pallas_call | solution.py:97
  42.5 7.7 %collective-permute-done.15.refs_2_ = bf16[512,896]{1,0:T(8,128)(2,1)} collective-permute-done((bf16[512,896]{1,0:T(8,128)(2,1)}, bf16[512,896]{1,0:T(8,128)(2,1)}, u32[]{:S(2)}, u32[]{:S(2)}) %collective-permute-start.15) | collective-permute-done | bytes 917536 | tf_op jit(solution)/shard_map/ppermute | solution.py:358
  50.2 9.3 %lookup.6.kept_ref = bf16[1024,896]{1,0:T(8,128)(2,1)} custom-call(s32[4096]{0:T(1024)} %bitcast.130, s32[16]{0:T(128)} %reduce_sum.18.count_ref, s32[128,32]{1,0:T(8,128)} %broadcast_add_fusion.code_ref, bf16[37984,896]{1,0:T(8,128)(2,1)} %table_ref.7), custom_call_target="tpu_custom_call" | custom-call | flops 5120000000 | bytes 16515072 | tf_op jit(solution)/shard_map/lookup/pallas_call | solution.py:97
  60.1 9.7 %collective-permute-done.7.refs_2_ = bf16[512,896]{1,0:T(8,128)(2,1)} collective-permute-done((bf16[512,896]{1,0:T(8,128)(2,1)S(1)}, bf16[512,896]{1,0:T(8,128)(2,1)}, u32[]{:S(2)}, u32[]{:S(2)}) %collective-permute-start.7) | collective-permute-done | bytes 917536 | tf_op jit(solution)/shard_map/ppermute | solution.py:358
  72.8 16.0 %collective-permute-done.1.away_ref = bf16[512,896]{1,0:T(8,128)(2,1)} collective-permute-done((bf16[512,896]{1,0:T(8,128)(2,1)}, bf16[512,896]{1,0:T(8,128)(2,1)}, u32[]{:S(2)}, u32[]{:S(2)}) %collective-permute-start.1) | collective-permute-done | bytes 917536 | tf_op jit(solution)/shard_map/ppermute | solution.py:380
  101.1 11.3 %collective-permute-done.10.away_ref = bf16[512,896]{1,0:T(8,128)(2,1)} collective-permute-done((bf16[512,896]{1,0:T(8,128)(2,1)}, bf16[512,896]{1,0:T(8,128)(2,1)}, u32[]{:S(2)}, u32[]{:S(2)}) %collective-permute-start.10) | collective-permute-done | bytes 917536 | tf_op jit(solution)/shard_map/ppermute | solution.py:380
  117.0 15.0 %collective-permute-done.3.refs_2_ = bf16[512,896]{1,0:T(8,128)(2,1)} collective-permute-done((bf16[512,896]{1,0:T(8,128)(2,1)}, bf16[512,896]{1,0:T(8,128)(2,1)}, u32[]{:S(2)}, u32[]{:S(2)}) %collective-permute-start.3) | collective-permute-done | bytes 917536 | tf_op jit(solution)/shard_map/ppermute | solution.py:358
  132.0 10.2 %fusion.47 = f32[2048,1216]{0,1:T(8,128)} fusion(bf16[2048,896]{1,0:T(8,128)(2,1)} %join.5, bf16[1216,896]{1,0:T(8,128)(2,1)} %param.10), kind=kOutput, calls=%fused_computation.96 | convolution fusion | flops 4462739456 | bytes 15810560 | tf_op jit(solution)/shard_map/dot_general | solution.py:335
  142.7 7.4 %collective-permute-done.12.refs_2_ = bf16[512,896]{1,0:T(8,128)(2,1)} collective-permute-done((bf16[512,896]{1,0:T(8,128)(2,1)}, bf16[512,896]{1,0:T(8,128)(2,1)}, u32[]{:S(2)}, u32[]{:S(2)}) %collective-permute-start.12) | collective-permute-done | bytes 917536 | tf_op jit(solution)/shard_map/ppermute | solution.py:358
  153.8 7.8 %convolution_convert_fusion.1 = bf16[2048,1216]{0,1:T(8,128)(2,1)S(1)} fusion(bf16[2048,896]{1,0:T(8,128)(2,1)} %join.4, bf16[896,1216]{0,1:T(8,128)(2,1)S(1)} %copy-done), kind=kOutput, calls=%fused_computation.39 | convolution fusion | flops 4465229824 | bytes 10829824 | tf_op jit(solution)/shard_map/dot_general | solution.py:335
  161.7 11.9 %fusion.4 = bf16[2048,1216]{0,1:T(8,128)(2,1)S(1)} fusion(bf16[2048,1216]{0,1:T(8,128)(2,1)S(1)} %convolution_convert_fusion.1, bf16[2048,896]{1,0:T(8,128)(2,1)S(1)} %copy-done.26, bf16[1216,896]{1,0:T(8,128)(2,1)S(1)} %copy-done.17), kind=kOutput, calls=%fused_computation.17 | convolution fusion | flops 4515037184 | bytes 15810560 | tf_op jit(solution)/shard_map/dot_general | solution.py:335
  173.6 5.8 %fusion.49 = f32[2048,896]{1,0:T(8,128)S(1)} fusion(bf16[2048,1216]{0,1:T(8,128)(2,1)S(1)} %fusion.4, bf16[896,1216]{0,1:T(8,128)(2,1)S(1)} %copy-done), kind=kOutput, calls=%fused_computation.98 | convolution fusion | flops 4462739456 | bytes 14499840 | tf_op jit(solution)/shard_map/dot_general | solution.py:335
  188.4 8.2 %convolution_convert_fusion = bf16[2048,1216]{0,1:T(8,128)(2,1)S(1)} fusion(bf16[2048,896]{1,0:T(8,128)(2,1)} %join.6, bf16[896,1216]{0,1:T(8,128)(2,1)S(1)} %copy-done), kind=kOutput, calls=%fused_computation.38 | convolution fusion | flops 4465229824 | bytes 10829824 | tf_op jit(solution)/shard_map/dot_general | solution.py:335
  196.7 6.3 %fusion.44 = f32[1216,896]{1,0:T(8,128)S(1)} fusion(bf16[2048,896]{1,0:T(8,128)(2,1)S(1)} %copy-done.28, bf16[2048,1216]{0,1:T(8,128)(2,1)S(1)} %convolution_convert_fusion), kind=kOutput, calls=%fused_computation.94 | convolution fusion | flops 4487643136 | bytes 13008896 | tf_op jit(solution)/shard_map/dot_general | solution.py:335
  203.0 7.9 %convolution_add_fusion.1 = f32[1216,896]{1,0:T(8,128)} fusion(f32[1216,896]{1,0:T(8,128)S(1)} %fusion.44, bf16[2048,896]{1,0:T(8,128)(2,1)S(1)} %copy-done.27, bf16[2048,1216]{0,1:T(8,128)(2,1)S(1)} %bitcast.137), kind=kOutput, calls=%fused_computation.42 | convolution fusion | flops 4488732672 | bytes 17367040 | tf_op jit(solution)/shard_map/dot_general | solution.py:335
  211.0 7.2 %fusion.7 = bf16[2048,1216]{0,1:T(8,128)(2,1)S(1)} fusion(bf16[2048,1216]{0,1:T(8,128)(2,1)S(1)} %convolution_convert_fusion, f32[2048,1216]{0,1:T(8,128)S(1)} %bitcast.118), kind=kLoop, calls=%fused_computation.20 | loop fusion | flops 52297728 | bytes 19922944 | tf_op jit(solution)/shard_map/convert_element_type | solution.py:404
  218.2 5.8 %fusion.48 = f32[2048,896]{1,0:T(8,128)S(1)} fusion(bf16[2048,1216]{0,1:T(8,128)(2,1)S(1)} %fusion.7, bf16[896,1216]{0,1:T(8,128)(2,1)S(1)} %copy-done), kind=kOutput, calls=%fused_computation.97 | convolution fusion | flops 4462739456 | bytes 14499840 | tf_op jit(solution)/shard_map/dot_general | solution.py:335
  227.3 7.8 %fusion.40 = f32[2048,896]{1,0:T(8,128)S(1)} fusion(bf16[1216,896]{1,0:T(8,128)(2,1)S(1)} %copy-done.18, bf16[2048,1216]{0,1:T(8,128)(2,1)S(1)} %bitcast.137), kind=kOutput, calls=%fused_computation.92 | convolution fusion | flops 4487643136 | bytes 14499840 | tf_op jit(solution)/shard_map/dot_general | solution.py:335
  235.1 4.9 fusion.30
  243.6 7.6 %fusion.42 = f32[2048,896]{1,0:T(8,128)S(1)} fusion(bf16[1216,896]{1,0:T(8,128)(2,1)S(1)} %copy-done.18, bf16[2048,1216]{0,1:T(8,128)(2,1)S(1)} %convolution_convert_fusion), kind=kOutput, calls=%fused_computation.93 | convolution fusion | flops 4487643136 | bytes 14499840 | tf_op jit(solution)/shard_map/dot_general | solution.py:335
  256.4 26.6 %collective-permute-done.24.away_ref = f32[512,896]{1,0:T(8,128)} collective-permute-done((f32[512,896]{1,0:T(8,128)S(1)}, f32[512,896]{1,0:T(8,128)}, u32[]{:S(2)}, u32[]{:S(2)}) %collective-permute-start.24) | collective-permute-done | bytes 1835040 | tf_op jit(solution)/shard_map/ppermute | solution.py:396
  288.8 32.5 %collective-permute-done.18.away_ref = f32[512,896]{1,0:T(8,128)S(1)} collective-permute-done((f32[512,896]{1,0:T(8,128)}, f32[512,896]{1,0:T(8,128)S(1)}, u32[]{:S(2)}, u32[]{:S(2)}) %collective-permute-start.18) | collective-permute-done | bytes 1835040 | tf_op jit(solution)/shard_map/ppermute | solution.py:396
  331.6 17.2 %collective-permute-done.19 = bf16[512,896]{1,0:T(8,128)(2,1)S(1)} collective-permute-done((bf16[512,896]{1,0:T(8,128)(2,1)}, bf16[512,896]{1,0:T(8,128)(2,1)S(1)}, u32[]{:S(2)}, u32[]{:S(2)}) %collective-permute-start.19) | collective-permute-done | bytes 917536 | tf_op jit(solution)/shard_map/ppermute | solution.py:437
  355.5 6.8 %sort.10 = (s32[8192]{0:T(1024)S(1)}, s32[8192]{0:T(1024)}) sort(s32[8192]{0:T(1024)S(1)} %iota_add_fusion, s32[8192]{0:T(1024)S(1)} %iota.20), dimensions={0}, to_apply=%region_1.2 | sort | flops 106496 | bytes 131072 | tf_op jit(solution)/shard_map/sort | solution.py:297
  380.3 30.3 %collective-permute-done.20.refs_6_ = bf16[1024,896]{1,0:T(8,128)(2,1)} collective-permute-done((bf16[1024,896]{1,0:T(8,128)(2,1)S(1)}, bf16[1024,896]{1,0:T(8,128)(2,1)}, u32[]{:S(2)}, u32[]{:S(2)}) %collective-permute-start.20) | collective-permute-done | bytes 1835040 | tf_op jit(solution)/shard_map/ppermute | solution.py:444
  410.6 5.3 fusion.50
  416.0 6.9 %convolution_add_fusion = f32[896,1216]{0,1:T(8,128)} fusion(f32[896,1216]{0,1:T(8,128)S(1)} %fusion.50, bf16[2048,1216]{0,1:T(8,128)(2,1)S(1)} %bitcast.135, bf16[2048,896]{1,0:T(8,128)(2,1)S(1)} %copy-done.24), kind=kOutput, calls=%fused_computation.41 | convolution fusion | flops 4463828992 | bytes 17367040 | tf_op jit(solution)/shard_map/dot_general | solution.py:335
  428.9 70.5 %table_grad.1 = f32[37984,896]{1,0:T(8,128)} custom-call(s32[20]{0:T(128)} %convert_reduce_fusion.start_ref, s32[8192]{0:T(1024)} %copy-done.15, s32[1]{0:T(128)} %bitcast.14.flip_ref, bf16[1024,896]{1,0:T(8,128)(2,1)} %pad_maximum_fusion.1.refs_0_, bf16[1024,896]{1,0:T(8,128)(2,1)} %copy-done.19, bf16[1024,896]{1,0:T(8,128)(2,1)} %collective-permute-done.27.refs_2_, ...), custom_call_target="tpu_custom_call" | custom-call | flops 60000002048 | bytes 136134656 | tf_op jit(solution)/shard_map/table_grad/pallas_call | solution.py:304
  500.7 56.3 %collective-permute-done.33 = f32[896,1216]{0,1:T(8,128)} collective-permute-done((f32[896,1216]{0,1:T(8,128)}, f32[896,1216]{0,1:T(8,128)}, u32[]{:S(2)}, u32[]{:S(2)}) %collective-permute-start.33) | collective-permute-done | bytes 4358176 | tf_op jit(solution)/shard_map/ppermute | solution.py:438
  557.0 6.1 %add.108 = f32[896,1216]{0,1:T(8,128)} add(f32[896,1216]{0,1:T(8,128)} %convolution_add_fusion, f32[896,1216]{0,1:T(8,128)} %collective-permute-done.33) | non-fusion elementwise | flops 1089536 | bytes 13074432 | tf_op jit(solution)/shard_map/add | solution.py:457
  (203 shorter events, 118.4 us)
Async XLA Ops:
  12.9 25.1 %collective-permute-start = (bf16[1024,896]{1,0:T(8,128)(2,1)}, bf16[1024,896]{1,0:T(8,128)(2,1)}, u32[]{:S(2)}, u32[]{:S(2)}) collective-permute-start(bf16[1024,896]{1,0:T(8,128)(2,1)} %lookup.5), channel_id=1, source_target_pairs={{0,1},{1,0},{2,3},{3,2},{4,5},{5,4},{6,7},{7,6}} | collective-permute-start | bytes 5505032 | tf_op jit(solution)/shard_map/ppermute | solution.py:377
  23.1 46.8 %collective-permute-start.9 = (bf16[1024,896]{1,0:T(8,128)(2,1)}, bf16[1024,896]{1,0:T(8,128)(2,1)}, u32[]{:S(2)}, u32[]{:S(2)}) collective-permute-start(bf16[1024,896]{1,0:T(8,128)(2,1)} %lookup.7), channel_id=1, source_target_pairs={{0,1},{1,0},{2,3},{3,2},{4,5},{5,4},{6,7},{7,6}} | collective-permute-start | bytes 5505032 | tf_op jit(solution)/shard_map/ppermute | solution.py:377
  25.7 24.5 %collective-permute-start.15 = (bf16[512,896]{1,0:T(8,128)(2,1)}, bf16[512,896]{1,0:T(8,128)(2,1)}, u32[]{:S(2)}, u32[]{:S(2)}) collective-permute-start(bf16[512,896]{1,0:T(8,128)(2,1)} %get-tuple-element.37.refs_0_), channel_id=1, source_target_pairs={{0,2},{2,0},{1,3},{3,1},{4,6},{6,4},{5,7},{7,5}} | collective-permute-start | bytes 2752520 | tf_op jit(solution)/shard_map/ppermute | solution.py:358
  28.7 41.2 %collective-permute-start.7 = (bf16[512,896]{1,0:T(8,128)(2,1)S(1)}, bf16[512,896]{1,0:T(8,128)(2,1)}, u32[]{:S(2)}, u32[]{:S(2)}) collective-permute-start(bf16[512,896]{1,0:T(8,128)(2,1)S(1)} %get-tuple-element.38.refs_0_), channel_id=1, source_target_pairs={{0,2},{2,0},{1,3},{3,1},{4,6},{6,4},{5,7},{7,5}} | collective-permute-start | bytes 2752520 | tf_op jit(solution)/shard_map/ppermute | solution.py:358
  40.5 48.3 %collective-permute-start.1 = (bf16[512,896]{1,0:T(8,128)(2,1)}, bf16[512,896]{1,0:T(8,128)(2,1)}, u32[]{:S(2)}, u32[]{:S(2)}) collective-permute-start(bf16[512,896]{1,0:T(8,128)(2,1)} %slice_add_fusion.1), channel_id=1, source_target_pairs={{0,2},{2,0},{1,3},{3,1},{4,6},{6,4},{5,7},{7,5}} | collective-permute-start | bytes 2752520 | tf_op jit(solution)/shard_map/ppermute | solution.py:380
  42.5 51.0 %collective-permute-start.14 = (bf16[512,896]{1,0:T(8,128)(2,1)}, bf16[512,896]{1,0:T(8,128)(2,1)}, u32[]{:S(2)}, u32[]{:S(2)}) collective-permute-start(bf16[512,896]{1,0:T(8,128)(2,1)} %get-tuple-element.37.refs_0_), channel_id=1, source_target_pairs={{0,1},{1,0},{2,3},{3,2},{4,5},{5,4},{6,7},{7,6}} | collective-permute-start | bytes 2752520 | tf_op jit(solution)/shard_map/ppermute | solution.py:359
  50.2 43.6 %collective-permute-start.16 = (bf16[512,896]{1,0:T(8,128)(2,1)}, bf16[512,896]{1,0:T(8,128)(2,1)}, u32[]{:S(2)}, u32[]{:S(2)}) collective-permute-start(bf16[512,896]{1,0:T(8,128)(2,1)} %collective-permute-done.15.refs_2_), channel_id=1, source_target_pairs={{0,1},{1,0},{2,3},{3,2},{4,5},{5,4},{6,7},{7,6}} | collective-permute-start | bytes 2752520 | tf_op jit(solution)/shard_map/ppermute | solution.py:360
  69.8 27.4 %collective-permute-start.6 = (bf16[512,896]{1,0:T(8,128)(2,1)S(1)}, bf16[512,896]{1,0:T(8,128)(2,1)}, u32[]{:S(2)}, u32[]{:S(2)}) collective-permute-start(bf16[512,896]{1,0:T(8,128)(2,1)S(1)} %get-tuple-element.38.refs_0_), channel_id=1, source_target_pairs={{0,1},{1,0},{2,3},{3,2},{4,5},{5,4},{6,7},{7,6}} | collective-permute-start | bytes 2752520 | tf_op jit(solution)/shard_map/ppermute | solution.py:359
  69.8 27.5 %collective-permute-start.8 = (bf16[512,896]{1,0:T(8,128)(2,1)}, bf16[512,896]{1,0:T(8,128)(2,1)}, u32[]{:S(2)}, u32[]{:S(2)}) collective-permute-start(bf16[512,896]{1,0:T(8,128)(2,1)} %collective-permute-done.7.refs_2_), channel_id=1, source_target_pairs={{0,1},{1,0},{2,3},{3,2},{4,5},{5,4},{6,7},{7,6}} | collective-permute-start | bytes 2752520 | tf_op jit(solution)/shard_map/ppermute | solution.py:360
  88.8 23.5 %collective-permute-start.10 = (bf16[512,896]{1,0:T(8,128)(2,1)}, bf16[512,896]{1,0:T(8,128)(2,1)}, u32[]{:S(2)}, u32[]{:S(2)}) collective-permute-start(bf16[512,896]{1,0:T(8,128)(2,1)} %slice_add_fusion), channel_id=1, source_target_pairs={{0,2},{2,0},{1,3},{3,1},{4,6},{6,4},{5,7},{7,5}} | collective-permute-start | bytes 2752520 | tf_op jit(solution)/shard_map/ppermute | solution.py:380
  93.5 38.5 %collective-permute-start.3 = (bf16[512,896]{1,0:T(8,128)(2,1)}, bf16[512,896]{1,0:T(8,128)(2,1)}, u32[]{:S(2)}, u32[]{:S(2)}) collective-permute-start(bf16[512,896]{1,0:T(8,128)(2,1)} %get-tuple-element.22.refs_0_), channel_id=1, source_target_pairs={{0,2},{2,0},{1,3},{3,1},{4,6},{6,4},{5,7},{7,5}} | collective-permute-start | bytes 2752520 | tf_op jit(solution)/shard_map/ppermute | solution.py:358
  101.0 49.1 %collective-permute-start.2 = (bf16[512,896]{1,0:T(8,128)(2,1)S(1)}, bf16[512,896]{1,0:T(8,128)(2,1)}, u32[]{:S(2)}, u32[]{:S(2)}) collective-permute-start(bf16[512,896]{1,0:T(8,128)(2,1)S(1)} %copy-done.23), channel_id=1, source_target_pairs={{0,1},{1,0},{2,3},{3,2},{4,5},{5,4},{6,7},{7,6}} | collective-permute-start | bytes 2752520 | tf_op jit(solution)/shard_map/ppermute | solution.py:359
  115.2 34.9 %collective-permute-start.12 = (bf16[512,896]{1,0:T(8,128)(2,1)}, bf16[512,896]{1,0:T(8,128)(2,1)}, u32[]{:S(2)}, u32[]{:S(2)}) collective-permute-start(bf16[512,896]{1,0:T(8,128)(2,1)} %get-tuple-element.23.refs_0_), channel_id=1, source_target_pairs={{0,2},{2,0},{1,3},{3,1},{4,6},{6,4},{5,7},{7,5}} | collective-permute-start | bytes 2752520 | tf_op jit(solution)/shard_map/ppermute | solution.py:358
  142.2 42.7 %collective-permute-start.11 = (bf16[512,896]{1,0:T(8,128)(2,1)}, bf16[512,896]{1,0:T(8,128)(2,1)}, u32[]{:S(2)}, u32[]{:S(2)}) collective-permute-start(bf16[512,896]{1,0:T(8,128)(2,1)} %get-tuple-element.23.refs_0_), channel_id=1, source_target_pairs={{0,1},{1,0},{2,3},{3,2},{4,5},{5,4},{6,7},{7,6}} | collective-permute-start | bytes 2752520 | tf_op jit(solution)/shard_map/ppermute | solution.py:359
  150.2 34.7 %collective-permute-start.13 = (bf16[512,896]{1,0:T(8,128)(2,1)}, bf16[512,896]{1,0:T(8,128)(2,1)}, u32[]{:S(2)}, u32[]{:S(2)}) collective-permute-start(bf16[512,896]{1,0:T(8,128)(2,1)} %collective-permute-done.12.refs_2_), channel_id=1, source_target_pairs={{0,1},{1,0},{2,3},{3,2},{4,5},{5,4},{6,7},{7,6}} | collective-permute-start | bytes 2752520 | tf_op jit(solution)/shard_map/ppermute | solution.py:360
  184.4 50.7 %collective-permute-start.23 = (f32[2,512,896]{2,1,0:T(8,128)}, f32[2,512,896]{2,1,0:T(8,128)}, u32[]{:S(2)}, u32[]{:S(2)}) collective-permute-start(f32[2,512,896]{2,1,0:T(8,128)} %slice_bitcast_fusion.1), channel_id=1, source_target_pairs={{0,1},{1,0},{2,3},{3,2},{4,5},{5,4},{6,7},{7,6}} | collective-permute-start | bytes 11010056 | tf_op jit(solution)/shard_map/ppermute | solution.py:391
  240.0 43.0 %collective-permute-start.24 = (f32[512,896]{1,0:T(8,128)S(1)}, f32[512,896]{1,0:T(8,128)}, u32[]{:S(2)}, u32[]{:S(2)}) collective-permute-start(f32[512,896]{1,0:T(8,128)S(1)} %fusion.30), channel_id=1, source_target_pairs={{0,2},{2,0},{1,3},{3,1},{4,6},{6,4},{5,7},{7,5}} | collective-permute-start | bytes 5505032 | tf_op jit(solution)/shard_map/ppermute | solution.py:396
  243.1 78.3 %collective-permute-start.18 = (f32[512,896]{1,0:T(8,128)}, f32[512,896]{1,0:T(8,128)S(1)}, u32[]{:S(2)}, u32[]{:S(2)}) collective-permute-start(f32[512,896]{1,0:T(8,128)} %fusion.31), channel_id=1, source_target_pairs={{0,2},{2,0},{1,3},{3,1},{4,6},{6,4},{5,7},{7,5}} | collective-permute-start | bytes 5505032 | tf_op jit(solution)/shard_map/ppermute | solution.py:396
  253.5 119.1 %collective-permute-start.5 = (f32[2,512,896]{2,1,0:T(8,128)}, f32[2,512,896]{2,1,0:T(8,128)}, u32[]{:S(2)}, u32[]{:S(2)}) collective-permute-start(f32[2,512,896]{2,1,0:T(8,128)} %slice_bitcast_fusion.3), channel_id=1, source_target_pairs={{0,1},{1,0},{2,3},{3,2},{4,5},{5,4},{6,7},{7,6}} | collective-permute-start | bytes 11010056 | tf_op jit(solution)/shard_map/ppermute | solution.py:391
  256.4 119.7 %collective-permute-start.31 = (f32[2,512,896]{2,1,0:T(8,128)}, f32[2,512,896]{2,1,0:T(8,128)}, u32[]{:S(2)}, u32[]{:S(2)}) collective-permute-start(f32[2,512,896]{2,1,0:T(8,128)} %slice_bitcast_fusion), channel_id=1, source_target_pairs={{0,1},{1,0},{2,3},{3,2},{4,5},{5,4},{6,7},{7,6}} | collective-permute-start | bytes 11010056 | tf_op jit(solution)/shard_map/ppermute | solution.py:391
  287.3 41.4 %collective-permute-start.25 = (bf16[512,896]{1,0:T(8,128)(2,1)}, bf16[512,896]{1,0:T(8,128)(2,1)S(1)}, u32[]{:S(2)}, u32[]{:S(2)}) collective-permute-start(bf16[512,896]{1,0:T(8,128)(2,1)} %norm_grad.3), channel_id=1, source_target_pairs={{0,4},{4,0},{1,5},{5,1},{2,6},{6,2},{3,7},{7,3}} | collective-permute-start | bytes 2752520 | tf_op jit(solution)/shard_map/ppermute | solution.py:424
  330.1 50.1 %collective-permute-start.27 = (bf16[1024,896]{1,0:T(8,128)(2,1)}, bf16[1024,896]{1,0:T(8,128)(2,1)}, u32[]{:S(2)}, u32[]{:S(2)}) collective-permute-start(bf16[1024,896]{1,0:T(8,128)(2,1)} %pad_maximum_fusion.1.refs_0_), channel_id=1, source_target_pairs={{0,2},{2,0},{1,3},{3,1},{4,6},{6,4},{5,7},{7,5}} | collective-permute-start | bytes 5505032 | tf_op jit(solution)/shard_map/ppermute | solution.py:444
  350.2 60.4 %collective-permute-start.20 = (bf16[1024,896]{1,0:T(8,128)(2,1)S(1)}, bf16[1024,896]{1,0:T(8,128)(2,1)}, u32[]{:S(2)}, u32[]{:S(2)}) collective-permute-start(bf16[1024,896]{1,0:T(8,128)(2,1)S(1)} %pad_maximum_fusion.refs_4_), channel_id=1, source_target_pairs={{0,2},{2,0},{1,3},{3,1},{4,6},{6,4},{5,7},{7,5}} | collective-permute-start | bytes 5505032 | tf_op jit(solution)/shard_map/ppermute | solution.py:444
  371.1 198.9 %collective-permute-start.34 = (f32[608,896]{1,0:T(8,128)}, f32[608,896]{1,0:T(8,128)S(1)}, u32[]{:S(2)}, u32[]{:S(2)}) collective-permute-start(f32[608,896]{1,0:T(8,128)} %slice.120), channel_id=1, source_target_pairs={{0,4},{4,0},{1,5},{5,1},{2,6},{6,2},{3,7},{7,3}} | collective-permute-start | bytes 6537224 | tf_op jit(solution)/shard_map/ppermute | solution.py:417
  379.7 43.1 %collective-permute-start.26 = (bf16[1024,896]{1,0:T(8,128)(2,1)}, bf16[1024,896]{1,0:T(8,128)(2,1)S(1)}, u32[]{:S(2)}, u32[]{:S(2)}) collective-permute-start(bf16[1024,896]{1,0:T(8,128)(2,1)} %pad_maximum_fusion.1.refs_0_), channel_id=1, source_target_pairs={{0,1},{1,0},{2,3},{3,2},{4,5},{5,4},{6,7},{7,6}} | collective-permute-start | bytes 5505032 | tf_op jit(solution)/shard_map/ppermute | solution.py:443
  379.7 43.6 %collective-permute-start.29 = (bf16[1024,896]{1,0:T(8,128)(2,1)S(1)}, bf16[1024,896]{1,0:T(8,128)(2,1)S(1)}, u32[]{:S(2)}, u32[]{:S(2)}) collective-permute-start(bf16[1024,896]{1,0:T(8,128)(2,1)S(1)} %pad_maximum_fusion.refs_4_), channel_id=1, source_target_pairs={{0,1},{1,0},{2,3},{3,2},{4,5},{5,4},{6,7},{7,6}} | collective-permute-start | bytes 5505032 | tf_op jit(solution)/shard_map/ppermute | solution.py:443
  380.2 44.6 %collective-permute-start.28 = (bf16[1024,896]{1,0:T(8,128)(2,1)}, bf16[1024,896]{1,0:T(8,128)(2,1)S(1)}, u32[]{:S(2)}, u32[]{:S(2)}) collective-permute-start(bf16[1024,896]{1,0:T(8,128)(2,1)} %collective-permute-done.27.refs_2_), channel_id=1, source_target_pairs={{0,1},{1,0},{2,3},{3,2},{4,5},{5,4},{6,7},{7,6}} | collective-permute-start | bytes 5505032 | tf_op jit(solution)/shard_map/ppermute | solution.py:445
  422.8 76.5 %collective-permute-start.36 = (f32[480,896]{1,0:T(8,128)}, f32[480,896]{1,0:T(8,128)}, u32[]{:S(2)}, u32[]{:S(2)}) collective-permute-start(f32[480,896]{1,0:T(8,128)} %slice.122), channel_id=1, source_target_pairs={{0,4},{4,0},{1,5},{5,1},{2,6},{6,2},{3,7},{7,3}} | collective-permute-start | bytes 5160968 | tf_op jit(solution)/shard_map/ppermute | solution.py:426
  423.4 133.6 %collective-permute-start.33 = (f32[896,1216]{0,1:T(8,128)}, f32[896,1216]{0,1:T(8,128)}, u32[]{:S(2)}, u32[]{:S(2)}) collective-permute-start(f32[896,1216]{0,1:T(8,128)} %convolution_add_fusion), channel_id=1, source_target_pairs={{0,4},{4,0},{1,5},{5,1},{2,6},{6,2},{3,7},{7,3}} | collective-permute-start | bytes 13074440 | tf_op jit(solution)/shard_map/ppermute | solution.py:438
  424.9 138.2 %collective-permute-start.21 = (f32[512,896]{1,0:T(8,128)}, f32[512,896]{1,0:T(8,128)S(1)}, u32[]{:S(2)}, u32[]{:S(2)}) collective-permute-start(f32[512,896]{1,0:T(8,128)} %fusion.32), channel_id=1, source_target_pairs={{0,2},{2,0},{1,3},{3,1},{4,6},{6,4},{5,7},{7,5}} | collective-permute-start | bytes 5505032 | tf_op jit(solution)/shard_map/ppermute | solution.py:396
  427.7 135.4 %collective-permute-start.32 = (f32[512,896]{1,0:T(8,128)}, f32[512,896]{1,0:T(8,128)}, u32[]{:S(2)}, u32[]{:S(2)}) collective-permute-start(f32[512,896]{1,0:T(8,128)} %fusion.25), channel_id=1, source_target_pairs={{0,2},{2,0},{1,3},{3,1},{4,6},{6,4},{5,7},{7,5}} | collective-permute-start | bytes 5505032 | tf_op jit(solution)/shard_map/ppermute | solution.py:396
  499.4 70.6 %collective-permute-start.35 = (f32[128,896]{1,0:T(8,128)}, f32[128,896]{1,0:T(8,128)S(1)}, u32[]{:S(2)}, u32[]{:S(2)}) collective-permute-start(f32[128,896]{1,0:T(8,128)} %slice.121), channel_id=1, source_target_pairs={{0,4},{4,0},{1,5},{5,1},{2,6},{6,2},{3,7},{7,3}} | collective-permute-start | bytes 1376264 | tf_op jit(solution)/shard_map/ppermute | solution.py:425
  (47 other events, 860.0 us)
